TPU v7x, 32 devices: a whole 2x2x4 slice. The times are simulated.
32 devices in a mesh: row: 8 (over y, x, core), col: 4 (over z).
Axes of the slice: x: 2, y: 2, z: 4, core: 2. Of those that a mesh axis runs over, the one named last changes fastest.
Arguments:
- velocity: float32 [3, 2, 128, 256, 256], P(None, None, 'row', 'col'), may hold values from -7.5 to 7.5
- accumulator: float32 [3, 2, 128, 256, 256], P(None, None, 'row', 'col'), may hold values from -6 to 6
- remesh_flag: int32 [128], P('row'), may hold values 0 or 1
- remesh_shift: int32 [128], P('row'), may hold values from -128 to 127
- viscosity: float32 [1], replicated, may hold values from 0.0003 to 0.0015
- shear: float32 [1], replicated, may hold values from 8 to 20
- clock: float32 [1], replicated, may hold values from 0 to 0.05
- step: float32 [1], replicated, may hold values from 0.004 to 0.01
Outputs:
- new_velocity: float32 [3, 2, 128, 256, 256], P(None, None, 'row', 'col')
- new_accumulator: float32 [3, 2, 128, 256, 256], P(None, None, 'row', 'col')
- spectra: float32 [2, 128], P(None, 'row')
All inputs are finite; a program needn't handle non-finite values. No bound on the sum of `remesh_flag` on one device may be relied on, other than what follows from the above.
Results may differ from a plain program's by a relative error of at most 0.0001.
Values sent between devices are 32-bit elements; how exact they have to be, the bound alone decides.
A program may use at most 192 MiB of HBM per device.

v0:
```python
import jax
import jax.numpy as jnp
import numpy as np
from jax import lax
from jax.experimental import pallas as pl
from jax.experimental.pallas import tpu as pltpu
from jax.sharding import PartitionSpec as P

NX = 256
NY = 256
NZ = 256


def tables(period):
    positions = np.arange(period)
    angles = (positions[:, None] * positions[None, :] % period) * (2.0 * np.pi / period)
    factor = 1.0 / np.sqrt(period)
    return np.cos(angles) * factor, np.sin(angles) * factor


def dot(formula, first, second):
    return jnp.einsum(
        formula, first, second, precision=lax.Precision.HIGH, preferred_element_type=jnp.float32
    )


def const(table):
    return jnp.asarray(np.ascontiguousarray(table), jnp.float32)


def make_tables(half_x, rows, cols):
    cos_x, sin_x = tables(NX)
    cos_y, sin_y = tables(NY)
    cos_z, sin_z = tables(NZ)
    block_y = NY // cols
    block_z = NZ // rows
    width_z = NZ // cols
    width_x = half_x // rows
    cy = cos_y.reshape(NY, cols, 1, block_y)
    sy = sin_y.reshape(NY, cols, 1, block_y)
    inv_y = np.stack([np.concatenate([cy, sy], 2), np.concatenate([-sy, cy], 2)])
    inv_y = inv_y.reshape(2 * NY, cols, 2 * block_y)
    cz = cos_z.reshape(rows, block_z, cols, width_z)
    sz = sin_z.reshape(rows, block_z, cols, width_z)
    inv_z = np.stack([cz, sz], 2)
    weight = np.where(np.arange(half_x) == 0, 1.0, 2.0)
    inv_x = np.stack([cos_x[:, :half_x] * weight, -sin_x[:, :half_x] * weight], 1)
    cx = cos_x[:half_x].reshape(rows, width_x, NX)
    sx = sin_x[:half_x].reshape(rows, width_x, NX)
    fwd_x = np.stack([cx, -sx], 1)
    cz = cos_z.reshape(cols, width_z, rows, block_z)
    sz = sin_z.reshape(cols, width_z, rows, block_z)
    fwd_z = np.stack([cz, sz], 2)
    cy = cos_y.reshape(cols, block_y, NY)
    sy = sin_y.reshape(cols, block_y, NY)
    fwd_y = np.concatenate(
        [np.concatenate([cy, -sy], 2), np.concatenate([sy, cy], 2)], 1
    )
    return [const(table) for table in (inv_y, inv_z, inv_x, fwd_x, fwd_z, fwd_y)]


def exchange(field, axis):
    return lax.all_to_all(field, axis, split_axis=0, concat_axis=0, tiled=True)


def to_grid(smooth, inv_y, inv_z, inv_x):
    part = dot("abk,kqj->qabj", smooth, inv_y)
    part = exchange(part, "col")
    half = part.shape[-1] // 2
    turned = jnp.concatenate([-part[..., half:], part[..., :half]], -1)
    part = dot("rzuhb,uhabk->razk", inv_z, jnp.stack([part, turned]))
    part = exchange(part, "row")
    rows, width, block_z, lanes = part.shape
    part = part.reshape(rows * width, block_z, lanes)
    mid = block_z // 2
    packed = jnp.stack(
        [
            jnp.concatenate([piece[:, :mid], piece[:, mid:]], -1)
            for piece in (part[..., :half], part[..., half:])
        ]
    )
    return dot("xtk,tkmj->xmj", inv_x, packed)


def to_modes(grid, fwd_x, fwd_z, fwd_y):
    part = exchange(dot("rtax,xmj->rtamj", fwd_x, grid), "row")
    half = part.shape[-1] // 2
    part = jnp.concatenate(
        [
            jnp.concatenate([part[:, t, ..., :half], part[:, t, ..., half:]], 2)
            for t in range(2)
        ],
        -1,
    )
    turned = jnp.concatenate([part[..., half:], -part[..., :half]], -1)
    part = dot("qbuhz,uhazk->qabk", fwd_z, jnp.stack([part, turned]))
    part = exchange(part, "col")
    return dot("habk,hkj->abj", part, fwd_y)


def geometry(base, real, shape):
    index_x = base[0] + pl.program_id(0)
    kx = index_x.astype(jnp.float32)
    iz = lax.broadcasted_iota(jnp.int32, shape, 0) + base[1]
    iz = jnp.where(2 * iz < NZ, iz, iz - NZ)
    iy = lax.broadcasted_iota(jnp.int32, shape, 1)
    iy = jnp.where(2 * iy < NY, iy, iy - NY)
    k0 = jnp.full(shape, kx, jnp.float32)
    k1 = iy.astype(jnp.float32) - real[4] * k0
    k2 = iz.astype(jnp.float32)
    ksq = k0 * k0 + k1 * k1 + k2 * k2
    inv = 1.0 / jnp.maximum(ksq, 1.0)
    keep = (3 * jnp.abs(iz) < NZ) & (3 * jnp.abs(iy) < NY) & (3.0 * k0 < float(NX))
    mask = jnp.where(keep, 1.0, 0.0)
    return (k0, k1, k2), ksq, inv, mask


def project(field, k, inv):
    along = (k[0] * field[0] + k[1] * field[1] + k[2] * field[2]) * inv
    return [field[c] - k[c] * along for c in range(3)]


def first_kernel(amount, base, real, vel, smooth, sums):
    shape = vel.shape[3:]
    full_y = shape[1]
    k, ksq, inv, mask = geometry(base, real, shape)
    shift = amount[pl.program_id(0)]
    v = [[pltpu.roll(vel[c, p, 0], shift, 1) for p in range(2)] for c in range(3)]
    stress = v[0][0] * v[1][0] + v[0][1] * v[1][1]
    energy = sum(v[c][p] * v[c][p] for c in range(3) for p in range(2))
    sums[0, 0:1] = jnp.sum(stress, axis=0, keepdims=True)
    sums[0, 1:2] = jnp.sum(ksq * energy, axis=0, keepdims=True)
    for p in range(2):
        out = project([v[c][p] for c in range(3)], k, inv)
        for c in range(3):
            smooth[c, 0, :, p * full_y : (p + 1) * full_y] = mask * out[c]


def last_kernel(amount, base, real, vel, acc, d0, d1, t01, t02, t12, new_vel, new_acc):
    shape = vel.shape[3:]
    full_y = shape[1]
    k, ksq, inv, mask = geometry(base, real, shape)
    shift = amount[pl.program_id(0)]
    viscosity, shear, step = real[0], real[1], real[3]
    coupling = 2.0 * shear * k[0] * inv
    for p in range(2):
        v = [pltpu.roll(vel[c, p, 0], shift, 1) for c in range(3)]
        old = [pltpu.roll(acc[c, p, 0], shift, 1) for c in range(3)]
        sign = mask if p == 0 else -mask
        other = slice((1 - p) * full_y, (2 - p) * full_y)
        e0, e1, e01, e02, e12 = [ref[0, :, other] for ref in (d0, d1, t01, t02, t12)]
        hat = [
            sign * (k[0] * e0 + k[1] * e01 + k[2] * e02),
            sign * (k[0] * e01 + k[1] * e1 + k[2] * e12),
            sign * (k[0] * e02 + k[1] * e12),
        ]
        hat = project(hat, k, inv)
        for c in range(3):
            rate = hat[c] + coupling * k[c] * v[1] - viscosity * ksq * v[c]
            if c == 0:
                rate = rate - shear * v[1]
            total = (-5.0 / 9.0) * old[c] + step * rate
            new_acc[c, p, 0] = total
            new_vel[c, p, 0] = v[c] + (15.0 / 16.0) * total


def body(velocity, accumulator, remesh_flag, remesh_shift, viscosity, shear, clock, step):
    rows = lax.axis_size("row")
    cols = lax.axis_size("col")
    _, _, width_x, width_z, full_y = velocity.shape
    amount = jnp.mod(-(remesh_flag * remesh_shift), full_y).astype(jnp.int32)
    base = jnp.stack(
        [lax.axis_index("row") * width_x, lax.axis_index("col") * width_z]
    ).astype(jnp.int32)
    real = jnp.concatenate([viscosity, shear, clock, step, shear * clock])
    state_spec = pl.BlockSpec((3, 2, 1, width_z, full_y), lambda i, *_: (0, 0, i, 0, 0))
    mode_spec = pl.BlockSpec((1, width_z, 2 * full_y), lambda i, *_: (i, 0, 0))
    params = pltpu.CompilerParams(
        dimension_semantics=("arbitrary",), vmem_limit_bytes=48 * 1024 * 1024
    )
    smooth, sums = pl.pallas_call(
        first_kernel,
        grid_spec=pltpu.PrefetchScalarGridSpec(
            num_scalar_prefetch=3,
            grid=(width_x,),
            in_specs=[state_spec],
            out_specs=[
                pl.BlockSpec((3, 1, width_z, 2 * full_y), lambda i, *_: (0, i, 0, 0)),
                pl.BlockSpec((1, 2, full_y), lambda i, *_: (i, 0, 0)),
            ],
        ),
        out_shape=[
            jax.ShapeDtypeStruct((3, width_x, width_z, 2 * full_y), jnp.float32),
            jax.ShapeDtypeStruct((width_x, 2, full_y), jnp.float32),
        ],
        compiler_params=params,
    )(amount, base, real, velocity)
    totals = lax.psum(jnp.sum(sums, axis=-1), "col")
    inv_y, inv_z, inv_x, fwd_x, fwd_z, fwd_y = make_tables(width_x * rows, rows, cols)
    u, v, w = [to_grid(smooth[c], inv_y, inv_z, inv_x) for c in range(3)]
    products = (u * u - w * w, v * v - w * w, u * v, u * w, v * w)
    modes = [to_modes(product, fwd_x, fwd_z, fwd_y) for product in products]
    new_velocity, new_accumulator = pl.pallas_call(
        last_kernel,
        grid_spec=pltpu.PrefetchScalarGridSpec(
            num_scalar_prefetch=3,
            grid=(width_x,),
            in_specs=[state_spec] * 2 + [mode_spec] * 5,
            out_specs=[state_spec] * 2,
        ),
        out_shape=[jax.ShapeDtypeStruct(velocity.shape, jnp.float32)] * 2,
        compiler_params=params,
    )(amount, base, real, velocity, accumulator, *modes)
    stress = totals[:, 0] / (NY * NZ)
    dissipation = 2.0 * viscosity[0] * totals[:, 1] / (NY * NZ)
    return new_velocity, new_accumulator, jnp.stack([stress, dissipation])


def solution(mesh):
    state = P(None, None, "row", "col", None)
    in_specs = (state, state, P("row"), P("row"), P(), P(), P(), P())
    out_specs = (state, state, P(None, "row"))
    return jax.shard_map(
        body, mesh=mesh, in_specs=in_specs, out_specs=out_specs, check_vma=False
    )
```

profile of v0, /device:TPU:18, one launch (start us, length us, event | category | flops | bytes accessed | tf_op | source)
XLA Modules:
  0.0 733.9 jit_solution(17298831703352190883)
XLA Ops:
  4.1 13.1 %shard_map.157 = (f32[3,16,64,512]{3,2,1,0:T(8,128)}, f32[16,2,256]{2,1,0:T(2,128)S(1)}) custom-call(s32[16]{0:T(128)S(1)} %and_select_fusion.amount, s32[2]{0:T(128)S(1)} %pad_add_fusion.base, f32[5]{0:T(128)S(1)} %concatenate.90.real, f32[3,2,16,64,256]{4,3,2,1,0:T(8,128)} %vel.3), custom_call_target="tpu_custom_call" | custom-call | tf_op jit(solution)/shard_map/pallas_call | solution.py:181
  32.2 40.0 %all-to-all-done.6 = f32[4,16,64,128]{3,2,1,0:T(8,128)S(1)} async-done(((f32[4,16,64,128]{3,2,1,0:T(8,128)}), f32[4,16,64,128]{3,2,1,0:T(8,128)S(1)}, u32[]{:S(2)}, u32[]{:S(2)}) %all-to-all-start.6) | async-done | bytes 2097184 | tf_op jit(solution)/shard_map/all_to_all | solution.py:63
  73.6 7.7 %all-to-all-start = ((f32[4,16,64,128]{3,2,1,0:T(8,128)}), f32[4,16,64,128]{3,2,1,0:T(8,128)}, u32[]{:S(2)}, u32[]{:S(2)}) async-start(f32[4,16,64,128]{3,2,1,0:T(8,128)} %copy.140), calls=%async_computation | async-start | bytes 4194304 | tf_op jit(solution)/shard_map/all_to_all | solution.py:63
  86.2 39.5 %all-to-all-done = f32[4,16,64,128]{3,2,1,0:T(8,128)} async-done(((f32[4,16,64,128]{3,2,1,0:T(8,128)}), f32[4,16,64,128]{3,2,1,0:T(8,128)}, u32[]{:S(2)}, u32[]{:S(2)}) %all-to-all-start) | async-done | bytes 2097184 | tf_op jit(solution)/shard_map/all_to_all | solution.py:63
  125.8 7.0 all-to-all-start.2
  139.9 37.4 %all-to-all-done.2 = f32[4,16,64,128]{3,2,1,0:T(8,128)S(1)} async-done(((f32[4,16,64,128]{3,2,1,0:T(8,128)}), f32[4,16,64,128]{3,2,1,0:T(8,128)S(1)}, u32[]{:S(2)}, u32[]{:S(2)}) %all-to-all-start.2) | async-done | bytes 2097184 | tf_op jit(solution)/shard_map/all_to_all | solution.py:63
  189.5 18.5 %all-to-all-done.1 = f32[8,16,32,128]{3,2,1,0:T(8,128)S(1)} async-done(((f32[8,16,32,128]{3,2,1,0:T(8,128)}), f32[8,16,32,128]{3,2,1,0:T(8,128)S(1)}, u32[]{:S(2)}, u32[]{:S(2)}) %all-to-all-start.1) | async-done | bytes 2097184 | tf_op jit(solution)/shard_map/all_to_all | solution.py:63
  220.4 18.7 %all-to-all-done.3 = f32[8,16,32,128]{3,2,1,0:T(8,128)} async-done(((f32[8,16,32,128]{3,2,1,0:T(8,128)}), f32[8,16,32,128]{3,2,1,0:T(8,128)}, u32[]{:S(2)}, u32[]{:S(2)}) %all-to-all-start.3) | async-done | bytes 2097184 | tf_op jit(solution)/shard_map/all_to_all | solution.py:63
  280.1 21.1 %all-to-all-done.12 = f32[8,2,16,16,128]{4,2,3,1,0:T(8,128)} async-done(((f32[8,2,16,16,128]{4,2,3,1,0:T(8,128)}), f32[8,2,16,16,128]{4,2,3,1,0:T(8,128)}, u32[]{:S(2)}, u32[]{:S(2)}) %all-to-all-start.12) | async-done | bytes 2097184 | tf_op jit(solution)/shard_map/all_to_all | solution.py:63
  301.3 6.1 all-to-all-start.4
  342.4 21.2 %all-to-all-done.10 = f32[8,2,16,16,128]{4,2,3,1,0:T(8,128)} async-done(((f32[8,2,16,16,128]{4,2,3,1,0:T(8,128)}), f32[8,2,16,16,128]{4,2,3,1,0:T(8,128)}, u32[]{:S(2)}, u32[]{:S(2)}) %all-to-all-start.10) | async-done | bytes 2097184 | tf_op jit(solution)/shard_map/all_to_all | solution.py:63
  373.3 21.2 %all-to-all-done.8 = f32[8,2,16,16,128]{4,2,3,1,0:T(8,128)} async-done(((f32[8,2,16,16,128]{4,2,3,1,0:T(8,128)}), f32[8,2,16,16,128]{4,2,3,1,0:T(8,128)}, u32[]{:S(2)}, u32[]{:S(2)}) %all-to-all-start.8) | async-done | bytes 2097184 | tf_op jit(solution)/shard_map/all_to_all | solution.py:63
  410.3 14.9 %all-to-all-done.14 = f32[8,2,16,16,128]{4,2,3,1,0:T(8,128)S(1)} async-done(((f32[8,2,16,16,128]{4,2,3,1,0:T(8,128)}), f32[8,2,16,16,128]{4,2,3,1,0:T(8,128)S(1)}, u32[]{:S(2)}, u32[]{:S(2)}) %all-to-all-start.14) | async-done | bytes 2097184 | tf_op jit(solution)/shard_map/all_to_all | solution.py:63
  425.2 7.7 %all-to-all-start.5 = ((f32[4,16,64,128]{3,2,1,0:T(8,128)}), f32[4,16,64,128]{3,2,1,0:T(8,128)}, u32[]{:S(2)}, u32[]{:S(2)}) async-start(f32[4,16,64,128]{3,2,1,0:T(8,128)} %copy.163), calls=%async_computation.5 | async-start | bytes 4194304 | tf_op jit(solution)/shard_map/all_to_all | solution.py:63
  442.1 36.2 %all-to-all-done.5 = f32[4,16,64,128]{3,2,1,0:T(8,128)} async-done(((f32[4,16,64,128]{3,2,1,0:T(8,128)}), f32[4,16,64,128]{3,2,1,0:T(8,128)}, u32[]{:S(2)}, u32[]{:S(2)}) %all-to-all-start.5) | async-done | bytes 2097184 | tf_op jit(solution)/shard_map/all_to_all | solution.py:63
  478.3 8.0 %all-to-all-start.13 = ((f32[4,16,64,128]{3,2,1,0:T(8,128)}), f32[4,16,64,128]{3,2,1,0:T(8,128)}, u32[]{:S(2)}, u32[]{:S(2)}) async-start(f32[4,16,64,128]{3,2,1,0:T(8,128)} %copy.190), calls=%async_computation.13 | async-start | bytes 4194304 | tf_op jit(solution)/shard_map/all_to_all | solution.py:63
  493.4 37.5 %all-to-all-done.13 = f32[4,16,64,128]{3,2,1,0:T(8,128)} async-done(((f32[4,16,64,128]{3,2,1,0:T(8,128)}), f32[4,16,64,128]{3,2,1,0:T(8,128)}, u32[]{:S(2)}, u32[]{:S(2)}) %all-to-all-start.13) | async-done | bytes 2097184 | tf_op jit(solution)/shard_map/all_to_all | solution.py:63
  530.8 7.0 all-to-all-start.15
  547.1 35.2 %all-to-all-done.15 = f32[4,16,64,128]{3,2,1,0:T(8,128)S(1)} async-done(((f32[4,16,64,128]{3,2,1,0:T(8,128)}), f32[4,16,64,128]{3,2,1,0:T(8,128)S(1)}, u32[]{:S(2)}, u32[]{:S(2)}) %all-to-all-start.15) | async-done | bytes 2097184 | tf_op jit(solution)/shard_map/all_to_all | solution.py:63
  583.6 7.9 %all-to-all-start.9 = ((f32[4,16,64,128]{3,2,1,0:T(8,128)}), f32[4,16,64,128]{3,2,1,0:T(8,128)}, u32[]{:S(2)}, u32[]{:S(2)}) async-start(f32[4,16,64,128]{3,2,1,0:T(8,128)} %copy.178), calls=%async_computation.9 | async-start | bytes 4194304 | tf_op jit(solution)/shard_map/all_to_all | solution.py:63
  600.8 35.2 %all-to-all-done.9 = f32[4,16,64,128]{3,2,1,0:T(8,128)} async-done(((f32[4,16,64,128]{3,2,1,0:T(8,128)}), f32[4,16,64,128]{3,2,1,0:T(8,128)}, u32[]{:S(2)}, u32[]{:S(2)}) %all-to-all-start.9) | async-done | bytes 2097184 | tf_op jit(solution)/shard_map/all_to_all | solution.py:63
  635.9 7.8 %all-to-all-start.11 = ((f32[4,16,64,128]{3,2,1,0:T(8,128)}), f32[4,16,64,128]{3,2,1,0:T(8,128)}, u32[]{:S(2)}, u32[]{:S(2)}) async-start(f32[4,16,64,128]{3,2,1,0:T(8,128)} %copy.184), calls=%async_computation.11 | async-start | bytes 4194304 | tf_op jit(solution)/shard_map/all_to_all | solution.py:63
  643.8 49.0 %psum.7 = f32[16,2]{1,0:T(8,128)S(1)} all-reduce(f32[16,2]{1,0:T(8,128)S(1)} %reduce_sum.9), channel_id=1, replica_groups=mesh['row'=8,'col'=4] {'col'}, use_global_device_ids=true, to_apply=%region_1.2 | all-reduce | flops 32 | bytes 256 | tf_op jit(solution)/shard_map/psum | solution.py:198
  715.0 18.8 %shard_map.158 = (f32[3,2,16,64,256]{4,3,2,1,0:T(8,128)}, f32[3,2,16,64,256]{4,3,2,1,0:T(8,128)}) custom-call(s32[16]{0:T(128)S(1)} %and_select_fusion.amount, s32[2]{0:T(128)S(1)} %pad_add_fusion.base, f32[5]{0:T(128)S(1)} %concatenate.90.real, f32[3,2,16,64,256]{4,3,2,1,0:T(8,128)} %vel.3, f32[3,2,16,64,256]{4,3,2,1,0:T(8,128)} %acc.1, ...), custom_call_target="tpu_custom_call" | custom-call | tf_op jit(solution)/shard_map/pallas_call | solution.py:203
  (138 shorter events, 213.7 us)
Async XLA Ops:
  4.1 13.1 %copy-start.7 = (f32[512,4,128,1]{2,0,1,3:T(8,128)S(1)}, f32[512,4,128,1]{2,0,1,3:T(8,128)}, u32[]{:S(2)}) copy-start(f32[512,4,128,1]{2,0,1,3:T(8,128)} %constant.56) | copy-start | bytes 3145732
  22.1 50.1 %all-to-all-start.6 = ((f32[4,16,64,128]{3,2,1,0:T(8,128)}), f32[4,16,64,128]{3,2,1,0:T(8,128)S(1)}, u32[]{:S(2)}, u32[]{:S(2)}) async-start(f32[4,16,64,128]{3,2,1,0:T(8,128)} %copy.164), calls=%async_computation.6 | async-start | bytes 4194304 | tf_op jit(solution)/shard_map/all_to_all | solution.py:63
  73.6 52.2 %all-to-all-start = ((f32[4,16,64,128]{3,2,1,0:T(8,128)}), f32[4,16,64,128]{3,2,1,0:T(8,128)}, u32[]{:S(2)}, u32[]{:S(2)}) async-start(f32[4,16,64,128]{3,2,1,0:T(8,128)} %copy.140), calls=%async_computation | async-start | bytes 4194304 | tf_op jit(solution)/shard_map/all_to_all | solution.py:63
  125.8 51.4 %all-to-all-start.2 = ((f32[4,16,64,128]{3,2,1,0:T(8,128)}), f32[4,16,64,128]{3,2,1,0:T(8,128)S(1)}, u32[]{:S(2)}, u32[]{:S(2)}) async-start(f32[4,16,64,128]{3,2,1,0:T(8,128)} %copy.149), calls=%async_computation.2 | async-start | bytes 4194304 | tf_op jit(solution)/shard_map/all_to_all | solution.py:63
  178.5 29.5 %all-to-all-start.1 = ((f32[8,16,32,128]{3,2,1,0:T(8,128)}), f32[8,16,32,128]{3,2,1,0:T(8,128)S(1)}, u32[]{:S(2)}, u32[]{:S(2)}) async-start(f32[8,16,32,128]{3,2,1,0:T(8,128)} %fusion.83), calls=%async_computation.1 | async-start | bytes 4194304 | tf_op jit(solution)/shard_map/all_to_all | solution.py:63
  208.1 31.0 %all-to-all-start.3 = ((f32[8,16,32,128]{3,2,1,0:T(8,128)}), f32[8,16,32,128]{3,2,1,0:T(8,128)}, u32[]{:S(2)}, u32[]{:S(2)}) async-start(f32[8,16,32,128]{3,2,1,0:T(8,128)} %fusion.82), calls=%async_computation.3 | async-start | bytes 4194304 | tf_op jit(solution)/shard_map/all_to_all | solution.py:63
  239.0 32.7 %all-to-all-start.7 = ((f32[8,16,32,128]{3,2,1,0:T(8,128)}), f32[8,16,32,128]{3,2,1,0:T(8,128)}, u32[]{:S(2)}, u32[]{:S(2)}) async-start(f32[8,16,32,128]{3,2,1,0:T(8,128)} %fusion.81), calls=%async_computation.7 | async-start | bytes 4194304 | tf_op jit(solution)/shard_map/all_to_all | solution.py:63
  247.4 5.0 copy-start.13
  262.6 1.7 copy-start.16
  262.6 1.7 copy-start.17
  271.8 29.5 %all-to-all-start.12 = ((f32[8,2,16,16,128]{4,2,3,1,0:T(8,128)}), f32[8,2,16,16,128]{4,2,3,1,0:T(8,128)}, u32[]{:S(2)}, u32[]{:S(2)}) async-start(f32[8,2,16,16,128]{4,2,3,1,0:T(8,128)} %fusion.33), calls=%async_computation.12 | async-start | bytes 4194304 | tf_op jit(solution)/shard_map/all_to_all | solution.py:63
  301.3 31.3 %all-to-all-start.4 = ((f32[8,2,16,16,128]{4,2,3,1,0:T(8,128)}), f32[8,2,16,16,128]{4,2,3,1,0:T(8,128)}, u32[]{:S(2)}, u32[]{:S(2)}) async-start(f32[8,2,16,16,128]{4,2,3,1,0:T(8,128)} %fusion.41), calls=%async_computation.4 | async-start | bytes 4194304 | tf_op jit(solution)/shard_map/all_to_all | solution.py:63
  322.2 2.4 copy-start.3
  332.6 31.0 %all-to-all-start.10 = ((f32[8,2,16,16,128]{4,2,3,1,0:T(8,128)}), f32[8,2,16,16,128]{4,2,3,1,0:T(8,128)}, u32[]{:S(2)}, u32[]{:S(2)}) async-start(f32[8,2,16,16,128]{4,2,3,1,0:T(8,128)} %fusion.35), calls=%async_computation.10 | async-start | bytes 4194304 | tf_op jit(solution)/shard_map/all_to_all | solution.py:63
  363.5 31.0 %all-to-all-start.8 = ((f32[8,2,16,16,128]{4,2,3,1,0:T(8,128)}), f32[8,2,16,16,128]{4,2,3,1,0:T(8,128)}, u32[]{:S(2)}, u32[]{:S(2)}) async-start(f32[8,2,16,16,128]{4,2,3,1,0:T(8,128)} %fusion.37), calls=%async_computation.8 | async-start | bytes 4194304 | tf_op jit(solution)/shard_map/all_to_all | solution.py:63
  394.5 30.6 %all-to-all-start.14 = ((f32[8,2,16,16,128]{4,2,3,1,0:T(8,128)}), f32[8,2,16,16,128]{4,2,3,1,0:T(8,128)S(1)}, u32[]{:S(2)}, u32[]{:S(2)}) async-start(f32[8,2,16,16,128]{4,2,3,1,0:T(8,128)} %fusion.31), calls=%async_computation.14 | async-start | bytes 4194304 | tf_op jit(solution)/shard_map/all_to_all | solution.py:63
  425.2 53.1 %all-to-all-start.5 = ((f32[4,16,64,128]{3,2,1,0:T(8,128)}), f32[4,16,64,128]{3,2,1,0:T(8,128)}, u32[]{:S(2)}, u32[]{:S(2)}) async-start(f32[4,16,64,128]{3,2,1,0:T(8,128)} %copy.163), calls=%async_computation.5 | async-start | bytes 4194304 | tf_op jit(solution)/shard_map/all_to_all | solution.py:63
  478.3 52.6 %all-to-all-start.13 = ((f32[4,16,64,128]{3,2,1,0:T(8,128)}), f32[4,16,64,128]{3,2,1,0:T(8,128)}, u32[]{:S(2)}, u32[]{:S(2)}) async-start(f32[4,16,64,128]{3,2,1,0:T(8,128)} %copy.190), calls=%async_computation.13 | async-start | bytes 4194304 | tf_op jit(solution)/shard_map/all_to_all | solution.py:63
  530.8 51.4 %all-to-all-start.15 = ((f32[4,16,64,128]{3,2,1,0:T(8,128)}), f32[4,16,64,128]{3,2,1,0:T(8,128)S(1)}, u32[]{:S(2)}, u32[]{:S(2)}) async-start(f32[4,16,64,128]{3,2,1,0:T(8,128)} %copy.196), calls=%async_computation.15 | async-start | bytes 4194304 | tf_op jit(solution)/shard_map/all_to_all | solution.py:63
  583.6 52.4 %all-to-all-start.9 = ((f32[4,16,64,128]{3,2,1,0:T(8,128)}), f32[4,16,64,128]{3,2,1,0:T(8,128)}, u32[]{:S(2)}, u32[]{:S(2)}) async-start(f32[4,16,64,128]{3,2,1,0:T(8,128)} %copy.178), calls=%async_computation.9 | async-start | bytes 4194304 | tf_op jit(solution)/shard_map/all_to_all | solution.py:63
  600.8 92.8 %copy-start.5 = (f32[4,128,512,1]{2,1,3,0:T(8,128)S(1)}, f32[4,128,512,1]{2,1,3,0:T(8,128)}, u32[]{:S(2)}) copy-start(f32[4,128,512,1]{2,1,3,0:T(8,128)} %constant.60) | copy-start | bytes 3145732
  635.9 74.0 %all-to-all-start.11 = ((f32[4,16,64,128]{3,2,1,0:T(8,128)}), f32[4,16,64,128]{3,2,1,0:T(8,128)}, u32[]{:S(2)}, u32[]{:S(2)}) async-start(f32[4,16,64,128]{3,2,1,0:T(8,128)} %copy.184), calls=%async_computation.11 | async-start | bytes 4194304 | tf_op jit(solution)/shard_map/all_to_all | solution.py:63
  697.0 5.0 copy-start.9
  710.0 5.0 copy-start
  (13 other events, 17.8 us)
where the time goes:
time: 744 us; the launch traced here: 734 us
  waiting for transfers between devices  382 us (51%)
  starting transfers between devices  102 us (14%)
  matrix products  77.3 us (10%)
  local copies, waits for them, and re-layouts  69.8 us (9%)
  blocking collectives  49 us (7%)
  Pallas kernels  31.9 us (4%)
  other arithmetic  18.2 us (2%)
    all_to_all x16, waiting for transfers between devices, exchange(): return lax.all_to_all(field, axis, split_axis=0, concat_axis=0, tiled=True)  382 us
    all_to_all x16, starting transfers between devices, exchange(): return lax.all_to_all(field, axis, split_axis=0, concat_axis=0, tiled=True)  102 us
    dot_general x24, matrix products, dot(): jnp.einsum(formula, first, second, precision=lax.Precision.HIGH, preferre...  77.3 us
    psum x1, blocking collectives, body(): totals = lax.psum(jnp.sum(sums, axis=-1), 'col')  49 us
    unnamed x54, local copies, waits for them, and re-layouts  29.3 us
    pallas_call x1, Pallas kernels, body(): pl.pallas_call(last_kernel, grid_spec=pltpu.PrefetchScalarGridSpec(num_sc...  18.8 us
  transfers between devices with their start and end apart: 16, of which 14 were waited for; matrix products, arithmetic and copies ran while one was open for 20% of the time, Pallas kernels for 0%

commit v1 on v0

v1 whole, which is shorter than its diff:
```python
import functools

import jax
import jax.numpy as jnp
import ml_dtypes
import numpy as np
from jax import lax
from jax.experimental import pallas as pl
from jax.experimental.pallas import tpu as pltpu
from jax.sharding import PartitionSpec as P

NX = 256
NY = 256
NZ = 256
LAG = 2
OCT = 8
VMEM_BYTES = 60 * 1024 * 1024
F32 = jnp.float32
BF16 = jnp.bfloat16


def tables(period):
    positions = np.arange(period)
    angles = (positions[:, None] * positions[None, :] % period) * (2.0 * np.pi / period)
    factor = 1.0 / np.sqrt(period)
    return np.cos(angles) * factor, np.sin(angles) * factor


def halves(table):
    table = np.ascontiguousarray(table).astype(np.float32)
    high = table.astype(ml_dtypes.bfloat16)
    low = (table - high.astype(np.float32)).astype(ml_dtypes.bfloat16)
    return [jnp.asarray(high), jnp.asarray(low)]


class Plan:
    def __init__(self, rows, cols, width_x, width_z):
        self.rows, self.cols = rows, cols
        self.wx, self.wz = width_x, width_z
        self.by, self.bz = NY // cols, NZ // rows
        self.live = sum(1 for k in range(rows * width_x) if 3 * k < NX)
        self.slots = -(-self.live // OCT) * OCT
        self.nh = width_x // OCT
        self.octs = self.slots // OCT
        alive = [3 * min(k, NZ - k) < NZ for k in range(NZ)]
        self.window = []
        self.offset = []
        total = 0
        for h in range(cols):
            inside = [k for k in range(width_z) if alive[h * width_z + k]]
            low = inside[0] // 8 * 8 if inside else 0
            high = -(-(inside[-1] + 1) // 8) * 8 if inside else 0
            self.window.append((low, high - low))
            self.offset.append(total)
            total += high - low
        self.kz = [
            h * width_z + low + k for h, (low, n) in enumerate(self.window) for k in range(n)
        ]
        self.stride = self.bz + 8 if self.bz % 16 == 0 else self.bz
        self.zg = max(1, min(self.bz, 256 // self.by))


def make_tables(plan):
    cos_x, sin_x = tables(NX)
    cos_y, sin_y = tables(NY)
    cos_z, sin_z = tables(NZ)
    cy = cos_y.reshape(NY, plan.cols, plan.by)
    sy = sin_y.reshape(NY, plan.cols, plan.by)
    inv_y = np.concatenate(
        [np.concatenate([cy, sy], 2), np.concatenate([-sy, cy], 2)], 0
    ).reshape(2 * NY, 2 * NY)
    inv_zc, inv_zs = cos_z[:, plan.kz], sin_z[:, plan.kz]
    kx = np.arange(plan.slots)
    weight = np.where(kx == 0, 1.0, 2.0) * (kx < plan.live)
    cx, sx = cos_x[:, : plan.slots], sin_x[:, : plan.slots]
    inv_x = np.concatenate([cx * weight, -sx * weight], 1)
    keep = (kx < plan.live)[:, None]
    fwd_x = np.concatenate([cx.T * keep, -sx.T * keep], 0)
    cy = cos_y.reshape(plan.cols, plan.by, NY)
    sy = sin_y.reshape(plan.cols, plan.by, NY)
    fwd_y = np.concatenate(
        [np.concatenate([cy, -sy], 2), np.concatenate([sy, cy], 2)], 1
    ).reshape(2 * NY, 2 * NY)
    return {
        "inv_y": halves(inv_y),
        "inv_z": halves(inv_zc) + halves(inv_zs),
        "inv_x": halves(inv_x),
        "fwd_x": halves(fwd_x),
        "fwd_z": halves(inv_zc.T) + halves(inv_zs.T),
        "fwd_y": halves(fwd_y),
    }


def split(value):
    high = value.astype(BF16)
    return high, (value - high.astype(F32)).astype(BF16)


def mul(a, b):
    return jnp.dot(a, b, preferred_element_type=F32)


def dot3(ah, al, bh, bl):
    return mul(ah, bh) + mul(ah, bl) + mul(al, bh)


def geometry(kx, first_z, real, shape):
    iz = lax.broadcasted_iota(jnp.int32, shape, 0) + first_z
    iz = jnp.where(2 * iz < NZ, iz, iz - NZ)
    iy = lax.broadcasted_iota(jnp.int32, shape, 1)
    iy = jnp.where(2 * iy < NY, iy, iy - NY)
    k0 = jnp.full(shape, kx.astype(F32), F32)
    k1 = iy.astype(F32) - real[4] * k0
    k2 = iz.astype(F32)
    ksq = k0 * k0 + k1 * k1 + k2 * k2
    inv = 1.0 / jnp.maximum(ksq, 1.0)
    keep = (3 * jnp.abs(iz) < NZ) & (3 * jnp.abs(iy) < NY) & (3.0 * k0 < float(NX))
    return (k0, k1, k2), ksq, inv, keep


def project(field, k, inv):
    along = (k[0] * field[0] + k[1] * field[1] + k[2] * field[2]) * inv
    return [field[c] - k[c] * along for c in range(3)]


def greet(rows, cols):
    row, col = lax.axis_index("row"), lax.axis_index("col")
    barrier = pltpu.get_barrier_semaphore()
    for k in range(1, cols):
        pl.semaphore_signal(
            barrier, inc=1, device_id={"col": (col + k) % cols},
            device_id_type=pl.DeviceIdType.MESH,
        )
    for k in range(1, rows):
        pl.semaphore_signal(
            barrier, inc=1, device_id={"row": (row + k) % rows},
            device_id_type=pl.DeviceIdType.MESH,
        )
    pl.semaphore_wait(barrier, rows + cols - 2)


def remote(src, dst, send, recv, axis, index):
    return pltpu.make_async_remote_copy(
        src_ref=src, dst_ref=dst, send_sem=send, recv_sem=recv,
        device_id={axis: index}, device_id_type=pl.DeviceIdType.MESH,
    )


def backward_part(
    plan, grid_in, ixh, ixl, fxh, fxl, ch, cl, sh, sl,
    modes, blocks, spans, lines, row_send, row_recv, col_send, col_recv,
):
    row, col = lax.axis_index("row"), lax.axis_index("col")
    rows, cols, by, bz, zg = plan.rows, plan.cols, plan.by, plan.bz, plan.zg
    slots, octs, nh = plan.slots, plan.octs, plan.nh
    chunks = nh * 5

    def grid_step(g, carry):
        fields = []
        for c in range(3):
            lines_z = [
                grid_in[c, pl.ds(g * zg + z, slots, stride=plan.stride), :]
                for z in range(zg)
            ]
            packed = jnp.concatenate(
                [
                    jnp.concatenate([f[:, :by] for f in lines_z], 1),
                    jnp.concatenate([f[:, by:] for f in lines_z], 1),
                ],
                0,
            )
            high, low = split(packed)
            fields.append(dot3(ixh[...], ixl[...], high, low))
        u, v, w = fields
        ww = w * w
        for p, product in enumerate((u * u - ww, v * v - ww, u * v, u * w, v * w)):
            high, low = split(product)
            made = dot3(fxh[...], fxl[...], high, low)
            for z in range(zg):
                line = jnp.concatenate(
                    [
                        made[:slots, z * by : (z + 1) * by],
                        made[slots:, z * by : (z + 1) * by],
                    ],
                    1,
                )
                for o in range(octs):
                    blocks[
                        p, o, pl.ds(pl.multiple_of((g * zg + z) * OCT, OCT), OCT), :
                    ] = line[o * OCT : (o + 1) * OCT]
        return carry

    lax.fori_loop(0, bz // zg, grid_step, 0)

    def row_copy(c, o, s, source):
        return remote(
            blocks.at[c % 5, o],
            spans.at[c, pl.ds(source * bz * OCT, bz * OCT), :],
            row_send.at[c, s], row_recv.at[c, source], "row", s,
        )

    def live(s, c):
        return s * nh + c // 5 < octs

    def send(c, carry):
        for j in range(1, rows):
            s = (row + j) % rows

            @pl.when(live(s, c))
            def _():
                row_copy(c, s * nh + c // 5, s, row).start()

        return carry

    lax.fori_loop(0, chunks, send, 0)

    def col_copy(c, q, source):
        low, n = plan.window[q]
        off = plan.offset[q]
        return remote(
            lines.at[c, :, pl.ds(off, n), :],
            modes.at[c, source, :, pl.ds(low, n), :],
            col_send.at[c, q], col_recv.at[c, source], "col", q,
        )

    def keep_copy(c, q):
        low, n = plan.window[q]
        off = plan.offset[q]
        return pltpu.make_async_copy(
            lines.at[c, :, pl.ds(off, n), :],
            modes.at[c, col, :, pl.ds(low, n), :],
            col_send.at[c, q],
        )

    def span_step(c, carry):
        @pl.when(live(row, c))
        def _():
            spans[c, pl.ds(pl.multiple_of(row * bz * OCT, OCT), bz * OCT), :] = blocks[
                c % 5, row * nh + c // 5
            ]
            for j in range(1, rows):
                row_copy(c, 0, row, (row + j) % rows).wait_recv()
            for k in range(0, OCT, 2):
                x = [
                    spans[c, pl.ds(k + m, NZ, stride=OCT), :] for m in range(2)
                ]
                turned = [jnp.concatenate([f[:, by:], -f[:, :by]], 1) for f in x]
                xh, xl = split(jnp.concatenate(x, 1))
                th, tl = split(jnp.concatenate(turned, 1))
                made = dot3(ch[...], cl[...], xh, xl) + dot3(sh[...], sl[...], th, tl)
                for m in range(2):
                    lines[c, k + m] = made[:, m * 2 * by : (m + 1) * 2 * by]
            for j in range(1, cols):
                for q in range(cols):
                    if plan.window[q][1]:

                        @pl.when((col + j) % cols == q)
                        def _():
                            col_copy(c, q, col).start()

            for q in range(cols):
                if plan.window[q][1]:

                    @pl.when(col == q)
                    def _():
                        keep_copy(c, q).start()

        return carry

    lax.fori_loop(0, chunks, span_step, 0)

    def drain(c, carry):
        for j in range(1, rows):
            s = (row + j) % rows

            @pl.when(live(s, c))
            def _():
                row_copy(c, s * nh + c // 5, s, row).wait_send()

        @pl.when(live(row, c))
        def _():
            for q in range(cols):
                if plan.window[q][1]:

                    @pl.when(col == q)
                    def _():
                        keep_copy(c, q).wait()
                        for j in range(1, cols):
                            col_copy(c, q, (q + j) % cols).wait_recv()

                    @pl.when(col != q)
                    def _():
                        col_copy(c, q, col).wait_send()

        return carry

    lax.fori_loop(0, chunks, drain, 0)


def middle_kernel(
    plan, amount, real, vel, yh, yl, ch, cl, sh, sl,
    ixh, ixl, fxh, fxl, bch, bcl, bsh, bsl,
    modes, sums, grid_in, part, lines, spans, own, parts,
    col_send, col_recv, row_send, row_recv, sum_send, sum_recv, *back,
):
    step = pl.program_id(0)
    row, col = lax.axis_index("row"), lax.axis_index("col")
    rows, cols, wx, wz, by, bz = plan.rows, plan.cols, plan.wx, plan.wz, plan.by, plan.bz
    shape = (wz, NY)

    @pl.when(step == 0)
    def _():
        for c in range(3):
            for s in range(plan.live, plan.slots):
                grid_in[c, s * plan.stride : s * plan.stride + bz] = jnp.zeros(
                    (bz, 2 * by), F32
                )
        greet(rows, cols)

    def col_copy(i, h, q):
        low, n = plan.window[h]
        off = plan.offset[h]
        return remote(
            part.at[i, q, :, pl.ds(low, n), :], lines.at[i, :, pl.ds(off, n), :],
            col_send.at[i, q], col_recv.at[i, h], "col", q,
        )

    def row_copy(i, slot, r):
        return remote(
            spans.at[i, :, pl.ds(r * bz, bz), :],
            grid_in.at[:, pl.ds(slot * plan.stride, bz), :],
            row_send.at[i, r], row_recv.at[slot], "row", r,
        )

    def sum_copy(q):
        return remote(own, parts.at[col], sum_send.at[q], sum_recv.at[col], "col", q)

    @pl.when(step < wx)
    def _():
        i = step
        kx = row * wx + i
        k, ksq, inv, keep = geometry(kx, col * wz, real, shape)
        shift = amount[i]
        v = [[pltpu.roll(vel[c, p, 0], shift, 1) for p in range(2)] for c in range(3)]
        stress = v[0][0] * v[1][0] + v[0][1] * v[1][1]
        energy = sum(v[c][p] * v[c][p] for c in range(3) for p in range(2))
        own[i, 0:1] = jnp.sum(stress, axis=0, keepdims=True)
        own[i, 1:2] = jnp.sum(ksq * energy, axis=0, keepdims=True)

        @pl.when(kx < plan.live)
        def _():
            mask = jnp.where(keep, 1.0, 0.0)
            out = [project([v[c][p] for c in range(3)], k, inv) for p in range(2)]
            smooth = jnp.concatenate(
                [
                    jnp.concatenate([mask * out[0][c], mask * out[1][c]], 1)
                    for c in range(3)
                ],
                0,
            )
            high, low = split(smooth)
            made = dot3(high, low, yh[...], yl[...])
            for q in range(cols):
                for c in range(3):
                    part[i, q, c] = made[
                        c * wz : (c + 1) * wz, q * 2 * by : (q + 1) * 2 * by
                    ]
            for h in range(cols):
                if plan.window[h][1]:
                    low, n = plan.window[h]
                    off = plan.offset[h]

                    @pl.when(col == h)
                    def _():
                        lines[i, :, off : off + n, :] = part[i, h, :, low : low + n, :]
                        for j in range(1, cols):
                            q = (h + j) % cols
                            col_copy(i, h, q).start()

    @pl.when(step == wx)
    def _():
        for j in range(1, cols):
            sum_copy((col + j) % cols).start()

    @pl.when(step >= LAG)
    def _():
        i = step - LAG
        kx = row * wx + i

        @pl.when(kx < plan.live)
        def _():
            for h in range(cols):
                if plan.window[h][1]:

                    @pl.when(col != h)
                    def _():
                        col_copy(i, h, col).wait_recv()

            x = [lines[i, c] for c in range(3)]
            turned = [jnp.concatenate([-f[:, by:], f[:, :by]], 1) for f in x]
            xh, xl = split(jnp.concatenate(x, 1))
            th, tl = split(jnp.concatenate(turned, 1))
            made = dot3(ch[...], cl[...], xh, xl) + dot3(sh[...], sl[...], th, tl)
            for c in range(3):
                spans[i, c] = made[:, c * 2 * by : (c + 1) * 2 * by]
            for r in range(rows):

                @pl.when(row == r)
                def _():
                    for c in range(3):
                        grid_in[c, pl.ds(pl.multiple_of(kx * plan.stride, 8), bz)] = spans[
                            i, c, r * bz : (r + 1) * bz
                        ]

            for j in range(1, rows):
                row_copy(i, kx, (row + j) % rows).start()

    @pl.when(step == wx + LAG - 1)
    def _():
        def arrived(slot, carry):
            @pl.when(slot // wx != row)
            def _():
                row_copy(0, slot, row).wait_recv()

            return carry

        lax.fori_loop(0, plan.live, arrived, 0)
        backward_part(
            plan, grid_in, ixh, ixl, fxh, fxl, bch, bcl, bsh, bsl, modes, *back
        )

        def sent(i, carry):
            @pl.when(row * wx + i < plan.live)
            def _():
                for h in range(cols):
                    if plan.window[h][1]:

                        @pl.when(col == h)
                        def _():
                            for j in range(1, cols):
                                col_copy(i, h, (h + j) % cols).wait_send()

                for j in range(1, rows):
                    row_copy(i, row * wx + i, (row + j) % rows).wait_send()

            return carry

        lax.fori_loop(0, wx, sent, 0)
        total = own[...]
        for j in range(1, cols):
            h = (col + j) % cols
            remote(
                own, parts.at[h], sum_send.at[h], sum_recv.at[h], "col", h
            ).wait()
        parts[col] = total
        sums[...] = sum(parts[h] for h in range(cols))


def last_kernel(plan, amount, base, real, vel, acc, modes, fh, fl, new_vel, new_acc, hats):
    shape = vel.shape[3:]
    kx = base[0] + pl.program_id(0)
    k, ksq, inv, keep = geometry(kx, base[1], real, shape)
    shift = amount[pl.program_id(0)]
    viscosity, shear, step = real[0], real[1], real[3]
    coupling = 2.0 * shear * k[0] * inv
    wz = shape[0]

    @pl.when(kx < plan.live)
    def _():
        packed = jnp.concatenate(
            [
                jnp.concatenate([modes[0, p, h, 0] for h in range(plan.cols)], 1)
                for p in range(5)
            ],
            0,
        )
        high, low = split(packed)
        hats[...] = dot3(high, low, fh[...], fl[...])

    for p in range(2):
        v = [pltpu.roll(vel[c, p, 0], shift, 1) for c in range(3)]
        old = [pltpu.roll(acc[c, p, 0], shift, 1) for c in range(3)]
        other = slice((1 - p) * NY, (2 - p) * NY)
        e0, e1, e01, e02, e12 = [
            jnp.where(keep, hats[m * wz : (m + 1) * wz, other], 0.0) for m in range(5)
        ]
        sign = 1.0 if p == 0 else -1.0
        hat = [
            sign * (k[0] * e0 + k[1] * e01 + k[2] * e02),
            sign * (k[0] * e01 + k[1] * e1 + k[2] * e12),
            sign * (k[0] * e02 + k[1] * e12),
        ]
        hat = project(hat, k, inv)
        for c in range(3):
            rate = hat[c] + coupling * k[c] * v[1] - viscosity * ksq * v[c]
            if c == 0:
                rate = rate - shear * v[1]
            total = (-5.0 / 9.0) * old[c] + step * rate
            new_acc[c, p, 0] = total
            new_vel[c, p, 0] = v[c] + (15.0 / 16.0) * total


def body(velocity, accumulator, remesh_flag, remesh_shift, viscosity, shear, clock, step):
    rows = lax.axis_size("row")
    cols = lax.axis_size("col")
    _, _, wx, wz, full_y = velocity.shape
    plan = Plan(rows, cols, wx, wz)
    by, bz = plan.by, plan.bz
    table = make_tables(plan)
    amount = jnp.mod(-(remesh_flag * remesh_shift), full_y).astype(jnp.int32)
    base = jnp.stack([lax.axis_index("row") * wx, lax.axis_index("col") * wz]).astype(
        jnp.int32
    )
    real = jnp.concatenate([viscosity, shear, clock, step, shear * clock])
    whole = pl.BlockSpec(memory_space=pltpu.VMEM)
    kz = len(plan.kz)
    chunks = plan.nh * 5
    dma = pltpu.SemaphoreType.DMA
    modes, sums = pl.pallas_call(
        functools.partial(middle_kernel, plan),
        grid_spec=pltpu.PrefetchScalarGridSpec(
            num_scalar_prefetch=2,
            grid=(wx + LAG,),
            in_specs=[
                pl.BlockSpec(
                    (3, 2, 1, wz, full_y),
                    lambda i, *_: (0, 0, jnp.minimum(i, wx - 1), 0, 0),
                )
            ]
            + [whole] * 14,
            out_specs=[pl.BlockSpec(memory_space=pl.ANY), whole],
            scratch_shapes=[
                pltpu.VMEM((3, plan.slots * plan.stride, 2 * by), F32),
                pltpu.VMEM((wx, cols, 3, wz, 2 * by), F32),
                pltpu.VMEM((wx, 3, kz, 2 * by), F32),
                pltpu.VMEM((wx, 3, NZ, 2 * by), F32),
                pltpu.VMEM((wx, 2, full_y), F32),
                pltpu.VMEM((cols, wx, 2, full_y), F32),
                dma((wx, cols)),
                dma((wx, cols)),
                dma((wx, rows)),
                dma((plan.live,)),
                dma((cols,)),
                dma((cols,)),
                pltpu.VMEM((5, plan.octs, bz * OCT, 2 * by), F32),
                pltpu.VMEM((chunks, NZ * OCT, 2 * by), F32),
                pltpu.VMEM((chunks, OCT, kz, 2 * by), F32),
                dma((chunks, rows)),
                dma((chunks, rows)),
                dma((chunks, cols)),
                dma((chunks, cols)),
            ],
        ),
        out_shape=[
            jax.ShapeDtypeStruct((chunks, cols, OCT, wz, 2 * by), F32),
            jax.ShapeDtypeStruct((wx, 2, full_y), F32),
        ],
        compiler_params=pltpu.CompilerParams(
            dimension_semantics=("arbitrary",), vmem_limit_bytes=VMEM_BYTES,
            collective_id=0, has_side_effects=True,
        ),
    )(
        amount, real, velocity, *table["inv_y"], *table["inv_z"],
        *table["inv_x"], *table["fwd_x"], *table["fwd_z"],
    )
    modes = modes.reshape(plan.nh, 5, cols, OCT, wz, 2 * by)
    state_spec = pl.BlockSpec((3, 2, 1, wz, full_y), lambda i, *_: (0, 0, i, 0, 0))
    new_velocity, new_accumulator = pl.pallas_call(
        functools.partial(last_kernel, plan),
        grid_spec=pltpu.PrefetchScalarGridSpec(
            num_scalar_prefetch=3,
            grid=(wx,),
            in_specs=[state_spec] * 2
            + [
                pl.BlockSpec(
                    (1, 5, cols, 1, wz, 2 * by),
                    lambda i, *_: (i // OCT, 0, 0, i % OCT, 0, 0),
                )
            ]
            + [whole] * 2,
            out_specs=[state_spec] * 2,
            scratch_shapes=[pltpu.VMEM((5 * wz, 2 * full_y), F32)],
        ),
        out_shape=[jax.ShapeDtypeStruct(velocity.shape, F32)] * 2,
        compiler_params=pltpu.CompilerParams(
            dimension_semantics=("arbitrary",), vmem_limit_bytes=48 * 1024 * 1024
        ),
    )(amount, base, real, velocity, accumulator, modes, *table["fwd_y"])
    totals = jnp.sum(sums, axis=-1)
    stress = totals[:, 0] / (NY * NZ)
    dissipation = 2.0 * viscosity[0] * totals[:, 1] / (NY * NZ)
    return new_velocity, new_accumulator, jnp.stack([stress, dissipation])


def solution(mesh):
    state = P(None, None, "row", "col", None)
    in_specs = (state, state, P("row"), P("row"), P(), P(), P(), P())
    out_specs = (state, state, P(None, "row"))
    return jax.shard_map(
        body, mesh=mesh, in_specs=in_specs, out_specs=out_specs, check_vma=False
    )
```

time: 744 us -> 399 us (0.54)
  waiting for transfers between devices: 382 us -> 0 us
  Pallas kernels: 31.9 us -> 389 us
  starting transfers between devices: 102 us -> 0 us
  matrix products: 77.3 us -> 0 us
  local copies, waits for them, and re-layouts: 69.8 us -> 0.62 us
  blocking collectives: 49 us -> 0 us
  other arithmetic: 18.2 us -> 2.88 us
    all_to_all x16 -> x0, waiting for transfers between devices: 382 us -> none  [exchange(): return lax.all_to_all(field, axis, split_axis=0, concat_axis=0, tiled=True)]
    pallas_call x2, Pallas kernels: 31.9 us -> 389 us  [the longest x1 364 us: body(): pl.pallas_call(functools.partial(middle_kernel, plan), grid_spec=pltpu.Pr...]
    all_to_all x16 -> x0, starting transfers between devices: 102 us -> none  [exchange(): return lax.all_to_all(field, axis, split_axis=0, concat_axis=0, tiled=True)]
    dot_general x24 -> x0, matrix products: 77.3 us -> none  [dot(): jnp.einsum(formula, first, second, precision=lax.Precision.HIGH, preferre...]
    psum x1 -> x0, blocking collectives: 49 us -> none  [body(): totals = lax.psum(jnp.sum(sums, axis=-1), 'col')]
    unnamed x54 -> x8, local copies, waits for them, and re-layouts: 29.3 us -> 0.02 us
    another operation x17 -> x1, other arithmetic: 13 us -> 0.07 us  [body(): jnp.stack([lax.axis_index('row') * wx, lax.axis_index('col') * wz])]
    squeeze x5 -> x0, local copies, waits for them, and re-layouts: 12.6 us -> none  [to_modes(): part[:, t, ..., :half]]
  transfers between devices with their start and end apart: 16 -> 0, of which waited for: 14 -> 0; matrix products, arithmetic and copies ran while one was open for 20% -> 0% of each run, Pallas kernels for 0% -> 0%
where the time goes in v1:
time: 399 us; the launch traced here: 396 us
  Pallas kernels  389 us (97%)
    pallas_call x1, Pallas kernels, body(): pl.pallas_call(functools.partial(middle_kernel, plan), grid_spec=pltpu.Pr...  364 us
    pallas_call x1, Pallas kernels, body(): pl.pallas_call(functools.partial(last_kernel, plan), grid_spec=pltpu.Pref...  24.5 us

profile of v1, /device:TPU:18, one launch (start us, length us, event | category | flops | bytes accessed | tf_op | source)
XLA Modules:
  0.0 395.6 jit_solution(3883687769212186669)
XLA Ops:
  0.6 0.0 copy-start
  0.6 0.0 copy-start.1
  3.3 0.6 concatenate.3.real
  3.9 0.0 copy-start.2
  3.9 0.1 pad_add_fusion.base
  4.0 1.2 and_select_fusion.amount
  5.2 0.0 copy-start.3
  5.2 364.2 %shard_map.247 = (f32[10,4,8,64,128]{4,3,2,1,0:T(8,128)}, f32[16,2,256]{2,1,0:T(2,128)}) custom-call(s32[16]{0:T(128)} %and_select_fusion.amount, f32[5]{0:T(128)} %concatenate.3.real, f32[3,2,16,64,256]{4,3,2,1,0:T(8,128)} %vel.3, bf16[512,512]{1,0:T(8,128)(2,1)} %constant.69.clone.yh, bf16[512,512]{1,0:T(8,128)(2,1)} %constant.70.clone.yl, ...), custom_call_target="tpu_custom_call" | custom-call | tf_op jit(solution)/shard_map/pallas_call | solution.py:519
  369.4 0.8 reduce_sum.9
  370.3 0.2 fusion.2
  370.5 0.6 pad_maximum_fusion
  371.1 0.0 copy-done
  371.1 0.0 copy-done.1
  371.1 0.0 copy-done.2
  371.1 0.0 copy-done.3
  371.1 24.5 %shard_map.248 = (f32[3,2,16,64,256]{4,3,2,1,0:T(8,128)}, f32[3,2,16,64,256]{4,3,2,1,0:T(8,128)}) custom-call(s32[16]{0:T(128)S(1)} %copy-done.3, s32[2]{0:T(128)S(1)} %pad_add_fusion.base, f32[5]{0:T(128)S(1)} %copy-done.2, f32[3,2,16,64,256]{4,3,2,1,0:T(8,128)} %vel.3, f32[3,2,16,64,256]{4,3,2,1,0:T(8,128)} %acc.1, f32[2,5,4,8,64,128]{5,4,3,2,1,0:T(8,128)} %bitcast.6, ...), custom_call_target="tpu_custom_call" | custom-call | tf_op jit(solution)/shard_map/pallas_call | solution.py:568
Async XLA Ops:
  0.6 370.4 %copy-start = (bf16[512,512]{1,0:T(8,128)(2,1)S(1)}, bf16[512,512]{1,0:T(8,128)(2,1)}, u32[]{:S(2)}) copy-start(bf16[512,512]{1,0:T(8,128)(2,1)} %constant.84.clone.fl) | copy-start | bytes 1572868
  0.6 370.4 %copy-start.1 = (bf16[512,512]{1,0:T(8,128)(2,1)S(1)}, bf16[512,512]{1,0:T(8,128)(2,1)}, u32[]{:S(2)}) copy-start(bf16[512,512]{1,0:T(8,128)(2,1)} %constant.83.clone.fh) | copy-start | bytes 1572868
  3.9 367.1 %copy-start.2 = (f32[5]{0:T(128)S(1)}, f32[5]{0:T(128)}, u32[]{:S(2)}) copy-start(f32[5]{0:T(128)} %concatenate.3.real) | copy-start | bytes 64
  5.2 365.9 %copy-start.3 = (s32[16]{0:T(128)S(1)}, s32[16]{0:T(128)}, u32[]{:S(2)}) copy-start(s32[16]{0:T(128)} %and_select_fusion.amount) | copy-start | bytes 196

commit v2 on v1

--- a/solution.py
+++ b/solution.py
@@ -13,6 +13,7 @@
 NY = 256
 NZ = 256
 LAG = 2
+AHEAD = 1
 OCT = 8
 VMEM_BYTES = 60 * 1024 * 1024
 F32 = jnp.float32
@@ -212,7 +213,7 @@
 
         return carry
 
-    lax.fori_loop(0, chunks, send, 0)
+    lax.fori_loop(0, AHEAD, send, 0)
 
     def col_copy(c, q, source):
         low, n = plan.window[q]
@@ -233,6 +234,10 @@
         )
 
     def span_step(c, carry):
+        @pl.when(jnp.logical_not(live(row, c)) & (c + AHEAD < chunks))
+        def _():
+            send(c + AHEAD, 0)
+
         @pl.when(live(row, c))
         def _():
             spans[c, pl.ds(pl.multiple_of(row * bz * OCT, OCT), bz * OCT), :] = blocks[
@@ -240,6 +245,11 @@
             ]
             for j in range(1, rows):
                 row_copy(c, 0, row, (row + j) % rows).wait_recv()
+
+            @pl.when(c + AHEAD < chunks)
+            def _():
+                send(c + AHEAD, 0)
+
             for k in range(0, OCT, 2):
                 x = [
                     spans[c, pl.ds(k + m, NZ, stride=OCT), :] for m in range(2)

time: 399 us -> 349 us (0.87)
  Pallas kernels: 389 us -> 338 us
    pallas_call x1, Pallas kernels: 364 us -> 314 us  [body(): pl.pallas_call(functools.partial(middle_kernel, plan), grid_spec=pltpu.Pr...]
where the time goes in v2:
time: 349 us; the launch traced here: 345 us
  Pallas kernels  338 us (97%)
    pallas_call x1, Pallas kernels, body(): pl.pallas_call(functools.partial(middle_kernel, plan), grid_spec=pltpu.Pr...  314 us
    pallas_call x1, Pallas kernels, body(): pl.pallas_call(functools.partial(last_kernel, plan), grid_spec=pltpu.Pref...  24.5 us

profile of v2, /device:TPU:18, one launch (start us, length us, event | category | flops | bytes accessed | tf_op | source)
XLA Modules:
  0.0 345.0 jit_solution(925863272633712668)
XLA Ops:
  0.6 0.0 copy-start
  0.6 0.0 copy-start.1
  3.3 0.6 concatenate.3.real
  3.9 0.0 copy-start.2
  3.9 0.1 pad_add_fusion.base
  4.0 1.2 and_select_fusion.amount
  5.2 0.0 copy-start.3
  5.2 313.7 %shard_map.247 = (f32[10,4,8,64,128]{4,3,2,1,0:T(8,128)}, f32[16,2,256]{2,1,0:T(2,128)}) custom-call(s32[16]{0:T(128)} %and_select_fusion.amount, f32[5]{0:T(128)} %concatenate.3.real, f32[3,2,16,64,256]{4,3,2,1,0:T(8,128)} %vel.3, bf16[512,512]{1,0:T(8,128)(2,1)} %constant.69.clone.yh, bf16[512,512]{1,0:T(8,128)(2,1)} %constant.70.clone.yl, ...), custom_call_target="tpu_custom_call" | custom-call | tf_op jit(solution)/shard_map/pallas_call | solution.py:529
  318.9 0.8 reduce_sum.9
  319.7 0.2 fusion.2
  319.9 0.6 pad_maximum_fusion
  320.5 0.0 copy-done
  320.5 0.0 copy-done.1
  320.5 0.0 copy-done.2
  320.5 0.0 copy-done.3
  320.5 24.5 %shard_map.248 = (f32[3,2,16,64,256]{4,3,2,1,0:T(8,128)}, f32[3,2,16,64,256]{4,3,2,1,0:T(8,128)}) custom-call(s32[16]{0:T(128)S(1)} %copy-done.3, s32[2]{0:T(128)S(1)} %pad_add_fusion.base, f32[5]{0:T(128)S(1)} %copy-done.2, f32[3,2,16,64,256]{4,3,2,1,0:T(8,128)} %vel.3, f32[3,2,16,64,256]{4,3,2,1,0:T(8,128)} %acc.1, f32[2,5,4,8,64,128]{5,4,3,2,1,0:T(8,128)} %bitcast.6, ...), custom_call_target="tpu_custom_call" | custom-call | tf_op jit(solution)/shard_map/pallas_call | solution.py:578
Async XLA Ops:
  0.6 319.9 %copy-start = (bf16[512,512]{1,0:T(8,128)(2,1)S(1)}, bf16[512,512]{1,0:T(8,128)(2,1)}, u32[]{:S(2)}) copy-start(bf16[512,512]{1,0:T(8,128)(2,1)} %constant.84.clone.fl) | copy-start | bytes 1572868
  0.6 319.9 %copy-start.1 = (bf16[512,512]{1,0:T(8,128)(2,1)S(1)}, bf16[512,512]{1,0:T(8,128)(2,1)}, u32[]{:S(2)}) copy-start(bf16[512,512]{1,0:T(8,128)(2,1)} %constant.83.clone.fh) | copy-start | bytes 1572868
  3.9 316.6 %copy-start.2 = (f32[5]{0:T(128)S(1)}, f32[5]{0:T(128)}, u32[]{:S(2)}) copy-start(f32[5]{0:T(128)} %concatenate.3.real) | copy-start | bytes 64
  5.2 315.3 %copy-start.3 = (s32[16]{0:T(128)S(1)}, s32[16]{0:T(128)}, u32[]{:S(2)}) copy-start(s32[16]{0:T(128)} %and_select_fusion.amount) | copy-start | bytes 196

commit v3 on v1

v3 whole, which is shorter than its diff:
```python
import functools

import jax
import jax.numpy as jnp
import ml_dtypes
import numpy as np
from jax import lax
from jax.experimental import pallas as pl
from jax.experimental.pallas import tpu as pltpu
from jax.sharding import PartitionSpec as P

NX = 256
NY = 256
NZ = 256
LAG = 2
AHEAD = 2
DEPTH = 4
SLABS = 8
OCT = 8
VMEM_BYTES = 63 * 1024 * 1024
F32 = jnp.float32
BF16 = jnp.bfloat16


def tables(period):
    positions = np.arange(period)
    angles = (positions[:, None] * positions[None, :] % period) * (2.0 * np.pi / period)
    factor = 1.0 / np.sqrt(period)
    return np.cos(angles) * factor, np.sin(angles) * factor


def halves(table):
    table = np.ascontiguousarray(table).astype(np.float32)
    high = table.astype(ml_dtypes.bfloat16)
    low = (table - high.astype(np.float32)).astype(ml_dtypes.bfloat16)
    return [jnp.asarray(high), jnp.asarray(low)]


class Plan:
    def __init__(self, rows, cols, width_x, width_z):
        self.rows, self.cols = rows, cols
        self.wx, self.wz = width_x, width_z
        self.by, self.bz = NY // cols, NZ // rows
        self.live = sum(1 for k in range(rows * width_x) if 3 * k < NX)
        self.slots = -(-self.live // OCT) * OCT
        self.half = cols // 2
        alive = [3 * min(k, NZ - k) < NZ for k in range(NZ)]
        self.window = []
        self.offset = []
        total = 0
        for h in range(cols):
            inside = [k for k in range(width_z) if alive[h * width_z + k]]
            low = inside[0] // 8 * 8 if inside else 0
            high = -(-(inside[-1] + 1) // 8) * 8 if inside else 0
            self.window.append((low, high - low))
            self.offset.append(total)
            total += high - low
        self.kz = [
            h * width_z + low + k for h, (low, n) in enumerate(self.window) for k in range(n)
        ]
        self.side_rows = total // 2
        assert cols % 2 == 0 and self.offset[self.half] * 2 == total
        ky = [j if 2 * j < NY else j - NY for j in range(NY)]
        self.ky = [j for j in range(NY) if 3 * abs(ky[j]) < NY]
        self.ky_live = len(self.ky)
        self.lanes = 384
        self.stride = self.bz + 8 if self.bz % 16 == 0 else self.bz
        self.zg = max(1, min(self.bz, 256 // self.by))


def make_tables(plan):
    cos_x, sin_x = tables(NX)
    cos_y, sin_y = tables(NY)
    cos_z, sin_z = tables(NZ)
    cy = cos_y.reshape(NY, plan.cols, plan.by)
    sy = sin_y.reshape(NY, plan.cols, plan.by)
    inv_y = np.concatenate(
        [np.concatenate([cy, sy], 2), np.concatenate([-sy, cy], 2)], 0
    ).reshape(2 * NY, 2 * NY)
    inv_zc, inv_zs = cos_z[:, plan.kz], sin_z[:, plan.kz]
    kx = np.arange(plan.slots)
    weight = np.where(kx == 0, 1.0, 2.0) * (kx < plan.live)
    cx, sx = cos_x[:, : plan.slots], sin_x[:, : plan.slots]
    inv_x = np.concatenate([cx * weight, -sx * weight], 1)
    keep = (kx < plan.live)[:, None]
    fwd_x = np.concatenate([cx.T * keep, -sx.T * keep], 0)
    pad = [(0, 0), (0, 192 - plan.ky_live)]
    cy, sy = np.pad(cos_y[:, plan.ky], pad), np.pad(sin_y[:, plan.ky], pad)

    def lanes(re, im):
        return np.concatenate([re[:, :128], im[:, :128], re[:, 128:], im[:, 128:]], 1)

    block = []
    for h in range(plan.cols):
        y = slice(h * plan.by, (h + 1) * plan.by)
        block.append(np.concatenate([lanes(cy[y], -sy[y]), lanes(sy[y], cy[y])], 0))
    side_y = np.stack(
        [
            np.concatenate(
                [block[h // plan.half * plan.half + (h + j) % plan.half] for j in range(plan.half)], 0
            )
            for h in range(plan.cols)
        ]
    )
    signed = np.array([j if 2 * j < NY else j - NY for j in plan.ky], np.float64)
    signed = np.pad(signed, (0, 192 - plan.ky_live))[None]
    ky = np.repeat(lanes(signed, signed), 8, 0)
    kz = np.array([j if 2 * j < NZ else j - NZ for j in plan.kz], np.float64)
    kz = np.repeat(kz.reshape(2, plan.side_rows, 1)[::-1], plan.lanes, 2)
    return {
        "inv_y": halves(inv_y),
        "inv_z": halves(inv_zc) + halves(inv_zs),
        "inv_x": halves(inv_x),
        "fwd_x": halves(fwd_x),
        "fwd_z": halves(inv_zc.T) + halves(inv_zs.T),
        "side_y": halves(side_y),
        "ky": jnp.asarray(ky, F32),
        "kz_far": jnp.asarray(np.ascontiguousarray(kz), F32),
    }


def split(value):
    high = value.astype(BF16)
    return high, (value - high.astype(F32)).astype(BF16)


def mul(a, b):
    return jnp.dot(a, b, preferred_element_type=F32)


def dot3(ah, al, bh, bl):
    return mul(ah, bh) + mul(ah, bl) + mul(al, bh)


def geometry(kx, first_z, real, shape):
    iz = lax.broadcasted_iota(jnp.int32, shape, 0) + first_z
    iz = jnp.where(2 * iz < NZ, iz, iz - NZ)
    iy = lax.broadcasted_iota(jnp.int32, shape, 1)
    iy = jnp.where(2 * iy < NY, iy, iy - NY)
    k0 = jnp.full(shape, kx.astype(F32), F32)
    k1 = iy.astype(F32) - real[4] * k0
    k2 = iz.astype(F32)
    ksq = k0 * k0 + k1 * k1 + k2 * k2
    inv = 1.0 / jnp.maximum(ksq, 1.0)
    keep = (3 * jnp.abs(iz) < NZ) & (3 * jnp.abs(iy) < NY) & (3.0 * k0 < float(NX))
    return (k0, k1, k2), ksq, inv, keep


def project(field, k, inv):
    along = (k[0] * field[0] + k[1] * field[1] + k[2] * field[2]) * inv
    return [field[c] - k[c] * along for c in range(3)]


def greet(rows, cols):
    row, col = lax.axis_index("row"), lax.axis_index("col")
    barrier = pltpu.get_barrier_semaphore()
    for k in range(1, cols):
        pl.semaphore_signal(
            barrier, inc=1, device_id={"col": (col + k) % cols},
            device_id_type=pl.DeviceIdType.MESH,
        )
    for k in range(1, rows):
        pl.semaphore_signal(
            barrier, inc=1, device_id={"row": (row + k) % rows},
            device_id_type=pl.DeviceIdType.MESH,
        )
    pl.semaphore_wait(barrier, rows + cols - 2)


def remote(src, dst, send, recv, axis, index):
    return pltpu.make_async_remote_copy(
        src_ref=src, dst_ref=dst, send_sem=send, recv_sem=recv,
        device_id={axis: index}, device_id_type=pl.DeviceIdType.MESH,
    )


def reduce_modes(t, k0, k1, k2):
    t0, t1, t01, t02, t12 = t
    d0 = k0 * t0 + k1 * t01 + k2 * t02
    d1 = k0 * t01 + k1 * t1 + k2 * t12
    d2 = k0 * t02 + k1 * t12
    h2 = k0 * k0 + k2 * k2
    flat = h2 == 0.0
    first = jnp.where(flat, d0, k2 * d0 - k0 * d2)
    second = jnp.where(flat, d2, k1 * (k0 * d0 + k2 * d2) - h2 * d1)
    return first, second


def backward_part(
    plan, real, grid_in, ixh, ixl, fxh, fxl, ch, cl, sh, sl, yh, yl, ky, kz_far,
    out, blocks, spans, lines, near, relay, pairs, far,
    row_send, row_recv, near_send, near_recv, relay_send, relay_recv, far_send, far_recv,
):
    row, col = lax.axis_index("row"), lax.axis_index("col")
    rows, cols, by, bz, zg = plan.rows, plan.cols, plan.by, plan.bz, plan.zg
    wx, wz, slots, half, ns = plan.wx, plan.wz, plan.slots, plan.half, plan.side_rows
    side = col // half
    local = col % half
    other = 1 - side
    gate = jnp.where(side == 0, half - 1, half)
    far_gate = jnp.where(side == 0, half, half - 1)
    far_first = other * ns
    lk = ky.shape[1]

    def grid_step(g, carry):
        fields = []
        for c in range(3):
            lines_z = [
                grid_in[c, pl.ds(g * zg + z, slots, stride=plan.stride), :]
                for z in range(zg)
            ]
            packed = jnp.concatenate(
                [
                    jnp.concatenate([f[:, :by] for f in lines_z], 1),
                    jnp.concatenate([f[:, by:] for f in lines_z], 1),
                ],
                0,
            )
            high, low = split(packed)
            fields.append(dot3(ixh[...], ixl[...], high, low))
        u, v, w = fields
        ww = w * w
        for p, product in enumerate((u * u - ww, v * v - ww, u * v, u * w, v * w)):
            high, low = split(product)
            made = dot3(fxh[...], fxl[...], high, low)
            for z in range(zg):
                blocks[p, pl.ds(g * zg + z, slots, stride=plan.stride), :] = (
                    jnp.concatenate(
                        [
                            made[:slots, z * by : (z + 1) * by],
                            made[slots:, z * by : (z + 1) * by],
                        ],
                        1,
                    )
                )
        return carry

    lax.fori_loop(0, bz // zg, grid_step, 0)

    def row_copy(i, s, source):
        return remote(
            blocks.at[:, pl.ds((s * wx + i) * plan.stride, bz), :],
            spans.at[i, :, pl.ds(source * bz, bz), :],
            row_send.at[i % DEPTH, s], row_recv.at[i, source], "row", s,
        )

    def live(s, i):
        return s * wx + i < plan.live

    def row_wait(i):
        for j in range(1, rows):
            s = (row + j) % rows

            @pl.when(live(s, i))
            def _():
                row_copy(i, s, row).wait_send()

    def row_start(i):
        @pl.when(i >= DEPTH)
        def _():
            row_wait(i - DEPTH)

        for j in range(1, rows):
            s = (row + j) % rows

            @pl.when(live(s, i))
            def _():
                row_copy(i, s, row).start()

    for i in range(AHEAD):
        row_start(i)

    def near_copy(i, q, slot, mine):
        low, n = plan.window[q]
        return remote(
            lines.at[i % DEPTH, :, pl.ds(plan.offset[q], n), :],
            near.at[i, slot, :, pl.ds(low, n), :],
            near_send.at[i % DEPTH, slot], near_recv.at[i, slot], "col", mine,
        )

    def relay_copy(i, slot):
        return remote(
            lines.at[i % DEPTH, :, pl.ds(pl.multiple_of(far_first, 8), ns), :],
            relay.at[i, slot], relay_send.at[i % DEPTH], relay_recv.at[i, slot],
            "col", gate,
        )

    def far_copy(i, q, target):
        low, n = plan.window[q]
        first = plan.offset[q] - q // half * ns
        return remote(
            pairs.at[i % DEPTH, :, pl.ds(first, n), :],
            far.at[i, :, pl.ds(low, n), :],
            far_send.at[i % DEPTH, q], far_recv.at[i], "col", target,
        )

    def each_near(act):
        for j in range(1, half):
            q = side * half + (local + j) % half
            for h in range(cols):
                if plan.window[h][1]:

                    @pl.when(q == h)
                    def _():
                        act(h, half - j)

    def each_far(act):
        for h in range(cols):
            if plan.window[h][1]:

                @pl.when((col == gate) & (h // half == other))
                def _():
                    act(h)

    def wait_lines(i):
        each_near(lambda h, slot: near_copy(i, h, slot, h).wait_send())

        @pl.when(col != gate)
        def _():
            relay_copy(i, 1).wait_send()

    def wait_pairs(i):
        each_far(lambda h: far_copy(i, h, h).wait_send())

    def lines_step(i):
        spans[i, :, pl.ds(pl.multiple_of(row * bz, 8), bz), :] = blocks[
            :, pl.ds(pl.multiple_of((row * wx + i) * plan.stride, 8), bz), :
        ]
        for j in range(1, rows):
            row_copy(i, row, (row + j) % rows).wait_recv()

        @pl.when(i + AHEAD < wx)
        def _():
            row_start(i + AHEAD)

        @pl.when(i >= DEPTH)
        def _():
            wait_lines(i - DEPTH)

        x = [spans[i, p] for p in range(5)]
        turned = [jnp.concatenate([f[:, by:], -f[:, :by]], 1) for f in x]
        xh, xl = split(jnp.concatenate(x, 1))
        th, tl = split(jnp.concatenate(turned, 1))
        made = dot3(ch[...], cl[...], xh, xl) + dot3(sh[...], sl[...], th, tl)
        for p in range(5):
            lines[i % DEPTH, p] = made[:, p * 2 * by : (p + 1) * 2 * by]
        each_near(lambda h, slot: near_copy(i, h, slot, h).start())
        for j in range(1, half):

            @pl.when((local + j) % half == gate % half)
            def _():
                relay_copy(i, half - j).start()

        for h in range(cols):
            if plan.window[h][1]:
                low, n = plan.window[h]
                off = plan.offset[h]

                @pl.when(col == h)
                def _():
                    near[i, 0, :, low : low + n, :] = lines[
                        i % DEPTH, :, off : off + n, :
                    ]

    def transform(pieces, rows_in):
        high, low = split(jnp.concatenate([g.reshape(5 * rows_in, 2 * by) for g in pieces], 1))
        made = dot3(high, low, yh[...], yl[...])
        return [made[p * rows_in : (p + 1) * rows_in] for p in range(5)]

    def wave(i):
        k0 = jnp.full((1, lk), (row * wx + i).astype(F32), F32)
        return k0, ky[0:1] - real[4] * k0

    def relay_step(i):
        @pl.when(col == gate)
        def _():
            for j in range(1, half):
                relay_copy(i, j).wait_recv()

            @pl.when(i >= DEPTH)
            def _():
                wait_pairs(i - DEPTH)

            mine = lines[i % DEPTH, :, pl.ds(pl.multiple_of(far_first, 8), ns), :]
            t = transform([mine] + [relay[i, j] for j in range(1, half)], ns)
            k0, k1 = wave(i)
            first, second = reduce_modes(t, k0, k1, kz_far[...])
            pairs[i % DEPTH, 0] = first
            pairs[i % DEPTH, 1] = second
            each_far(lambda h: far_copy(i, h, h).start())

    def out_step(i):
        for h in range(cols):
            if plan.window[h][1]:

                @pl.when(col == h)
                def _():
                    for j in range(1, half):
                        near_copy(i, h, j, h).wait_recv()

        t = transform([near[i, j] for j in range(half)], wz)
        k0, k1 = wave(i)
        iz = lax.broadcasted_iota(jnp.int32, (wz, lk), 0) + col * wz
        k2 = jnp.where(2 * iz < NZ, iz, iz - NZ).astype(F32)
        first, second = reduce_modes(t, k0, k1, k2)
        for h in range(cols):
            if plan.window[h][1]:

                @pl.when(col == h)
                def _():
                    far_copy(i, h, far_gate).wait_recv()

        out[i, 0] = first + far[i, 0]
        out[i, 1] = second + far[i, 1]

    def span_step(t, carry):
        @pl.when((t + AHEAD < wx) & jnp.logical_not(live(row, t)))
        def _():
            row_start(t + AHEAD)

        @pl.when((t < wx) & live(row, t))
        def _():
            lines_step(t)

        @pl.when((t >= 1) & (t < wx + 1) & live(row, t - 1))
        def _():
            relay_step(t - 1)

        @pl.when((t >= 2) & live(row, t - 2))
        def _():
            out_step(t - 2)

        return carry

    lax.fori_loop(0, wx + 2, span_step, 0)

    def drain(i, carry):
        row_wait(i)
        return carry

    lax.fori_loop(wx - DEPTH, wx, drain, 0)

    def drain_lines(i, carry):
        @pl.when(live(row, i) & jnp.logical_not((i + DEPTH < wx) & live(row, i + DEPTH)))
        def _():
            wait_lines(i)
            wait_pairs(i)

        return carry

    lax.fori_loop(0, wx, drain_lines, 0)


def middle_kernel(
    plan, amount, real, vel, yh, yl, ch, cl, sh, sl,
    ixh, ixl, fxh, fxl, bch, bcl, bsh, bsl, byh, byl, ky, kz_far,
    out, sums, grid_in, part, lines, spans, own, parts,
    col_send, col_recv, row_send, row_recv, sum_send, sum_recv, *back,
):
    step = pl.program_id(0)
    row, col = lax.axis_index("row"), lax.axis_index("col")
    rows, cols, wx, wz, by, bz = plan.rows, plan.cols, plan.wx, plan.wz, plan.by, plan.bz
    shape = (wz, NY)

    @pl.when(step == 0)
    def _():
        for c in range(3):
            for s in range(plan.live, plan.slots):
                grid_in[c, s * plan.stride : s * plan.stride + bz] = jnp.zeros(
                    (bz, 2 * by), F32
                )
        greet(rows, cols)

    def col_copy(i, h, q):
        low, n = plan.window[h]
        off = plan.offset[h]
        return remote(
            part.at[i % SLABS, q, :, pl.ds(low, n), :], lines.at[i, :, pl.ds(off, n), :],
            col_send.at[i % SLABS, q], col_recv.at[i, h], "col", q,
        )

    def row_copy(i, slot, r):
        return remote(
            spans.at[i % DEPTH, :, pl.ds(r * bz, bz), :],
            grid_in.at[:, pl.ds(slot * plan.stride, bz), :],
            row_send.at[i % DEPTH, r], row_recv.at[slot], "row", r,
        )

    def sum_copy(q):
        return remote(own, parts.at[col], sum_send.at[q], sum_recv.at[col], "col", q)

    def wait_part(i):
        for h in range(cols):
            if plan.window[h][1]:

                @pl.when(col == h)
                def _():
                    for j in range(1, cols):
                        col_copy(i, h, (h + j) % cols).wait_send()

    def wait_spans(i):
        for j in range(1, rows):
            row_copy(i, row * wx + i, (row + j) % rows).wait_send()

    @pl.when(step < wx)
    def _():
        i = step
        kx = row * wx + i
        k, ksq, inv, keep = geometry(kx, col * wz, real, shape)
        shift = amount[i]
        v = [[pltpu.roll(vel[c, p, 0], shift, 1) for p in range(2)] for c in range(3)]
        stress = v[0][0] * v[1][0] + v[0][1] * v[1][1]
        energy = sum(v[c][p] * v[c][p] for c in range(3) for p in range(2))
        own[i, 0:1] = jnp.sum(stress, axis=0, keepdims=True)
        own[i, 1:2] = jnp.sum(ksq * energy, axis=0, keepdims=True)

        @pl.when(kx < plan.live)
        def _():
            mask = jnp.where(keep, 1.0, 0.0)
            flow = [project([v[c][p] for c in range(3)], k, inv) for p in range(2)]
            smooth = jnp.concatenate(
                [
                    jnp.concatenate([mask * flow[0][c], mask * flow[1][c]], 1)
                    for c in range(3)
                ],
                0,
            )
            high, low = split(smooth)
            made = dot3(high, low, yh[...], yl[...])

            @pl.when(i >= SLABS)
            def _():
                wait_part(i - SLABS)

            for q in range(cols):
                for c in range(3):
                    part[i % SLABS, q, c] = made[
                        c * wz : (c + 1) * wz, q * 2 * by : (q + 1) * 2 * by
                    ]
            for h in range(cols):
                if plan.window[h][1]:
                    low, n = plan.window[h]
                    off = plan.offset[h]

                    @pl.when(col == h)
                    def _():
                        lines[i, :, off : off + n, :] = part[
                            i % SLABS, h, :, low : low + n, :
                        ]
                        for j in range(1, cols):
                            col_copy(i, h, (h + j) % cols).start()

    @pl.when(step == wx)
    def _():
        for j in range(1, cols):
            sum_copy((col + j) % cols).start()

    @pl.when(step >= LAG)
    def _():
        i = step - LAG
        kx = row * wx + i

        @pl.when(kx < plan.live)
        def _():
            for h in range(cols):
                if plan.window[h][1]:

                    @pl.when(col != h)
                    def _():
                        col_copy(i, h, col).wait_recv()

            x = [lines[i, c] for c in range(3)]
            turned = [jnp.concatenate([-f[:, by:], f[:, :by]], 1) for f in x]
            xh, xl = split(jnp.concatenate(x, 1))
            th, tl = split(jnp.concatenate(turned, 1))
            made = dot3(ch[...], cl[...], xh, xl) + dot3(sh[...], sl[...], th, tl)

            @pl.when(i >= DEPTH)
            def _():
                wait_spans(i - DEPTH)

            for c in range(3):
                spans[i % DEPTH, c] = made[:, c * 2 * by : (c + 1) * 2 * by]
            grid_in[:, pl.ds(pl.multiple_of(kx * plan.stride, 8), bz), :] = spans[
                i % DEPTH, :, pl.ds(pl.multiple_of(row * bz, 8), bz), :
            ]
            for j in range(1, rows):
                row_copy(i, kx, (row + j) % rows).start()

    @pl.when(step == wx + LAG - 1)
    def _():
        def arrived(slot, carry):
            @pl.when(slot // wx != row)
            def _():
                row_copy(0, slot, row).wait_recv()

            return carry

        lax.fori_loop(0, plan.live, arrived, 0)
        backward_part(
            plan, real, grid_in, ixh, ixl, fxh, fxl, bch, bcl, bsh, bsl, byh, byl, ky,
            kz_far, out, *back
        )

        def sent(i, carry):
            def ends(depth):
                later = (i + depth < wx) & (row * wx + i + depth < plan.live)
                return (row * wx + i < plan.live) & jnp.logical_not(later)

            @pl.when(ends(SLABS))
            def _():
                wait_part(i)

            @pl.when(ends(DEPTH))
            def _():
                wait_spans(i)

            return carry

        lax.fori_loop(0, wx, sent, 0)
        total = own[...]
        for j in range(1, cols):
            h = (col + j) % cols
            remote(
                own, parts.at[h], sum_send.at[h], sum_recv.at[h], "col", h
            ).wait()
        parts[col] = total
        sums[...] = sum(parts[h] for h in range(cols))


def spread(pair, plan):
    ends = pair[:, 256:384]
    lane = lax.broadcasted_iota(jnp.int32, (pair.shape[0], NY), 1)
    rows = []
    for p in range(2):
        tail = ends if p == 0 else pltpu.roll(ends, 64, 1)
        packed = jnp.concatenate([pair[:, p * 128 : (p + 1) * 128], tail], 1)
        moved = pltpu.roll(packed, NY - plan.ky_live, 1)
        rows.append(jnp.where(2 * lane < NY, packed, moved))
    return rows


def last_kernel(plan, amount, base, real, vel, acc, modes, new_vel, new_acc):
    shape = vel.shape[3:]
    kx = base[0] + pl.program_id(0)
    k, ksq, inv, keep = geometry(kx, base[1], real, shape)
    shift = amount[pl.program_id(0)]
    viscosity, shear, step = real[0], real[1], real[3]
    coupling = 2.0 * shear * k[0] * inv
    h2 = k[0] * k[0] + k[2] * k[2]
    flat = h2 == 0.0
    ih2 = 1.0 / jnp.maximum(h2, 1.0)
    firsts = spread(modes[0, 0], plan)
    seconds = spread(modes[0, 1], plan)
    for p in range(2):
        v = [pltpu.roll(vel[c, p, 0], shift, 1) for c in range(3)]
        old = [pltpu.roll(acc[c, p, 0], shift, 1) for c in range(3)]
        sign = 1.0 if p == 0 else -1.0
        a = jnp.where(keep, sign * firsts[1 - p], 0.0)
        b = jnp.where(keep, sign * seconds[1 - p], 0.0)
        a1 = a * ih2
        b1 = b * inv
        b2 = k[1] * b1 * ih2
        hat = [
            jnp.where(flat, a, k[2] * a1 + k[0] * b2),
            jnp.where(flat, 0.0, -b1),
            jnp.where(flat, b, k[2] * b2 - k[0] * a1),
        ]
        for c in range(3):
            rate = hat[c] + coupling * k[c] * v[1] - viscosity * ksq * v[c]
            if c == 0:
                rate = rate - shear * v[1]
            total = (-5.0 / 9.0) * old[c] + step * rate
            new_acc[c, p, 0] = total
            new_vel[c, p, 0] = v[c] + (15.0 / 16.0) * total


def body(velocity, accumulator, remesh_flag, remesh_shift, viscosity, shear, clock, step):
    rows = lax.axis_size("row")
    cols = lax.axis_size("col")
    _, _, wx, wz, full_y = velocity.shape
    plan = Plan(rows, cols, wx, wz)
    by, bz, half, ns, lk = plan.by, plan.bz, plan.half, plan.side_rows, plan.lanes
    table = make_tables(plan)
    amount = jnp.mod(-(remesh_flag * remesh_shift), full_y).astype(jnp.int32)
    col = lax.axis_index("col")
    base = jnp.stack([lax.axis_index("row") * wx, col * wz]).astype(jnp.int32)
    real = jnp.concatenate([viscosity, shear, clock, step, shear * clock])
    side_y = [lax.dynamic_index_in_dim(t, col, 0, False) for t in table["side_y"]]
    kz_far = lax.dynamic_index_in_dim(table["kz_far"], col // half, 0, False)
    whole = pl.BlockSpec(memory_space=pltpu.VMEM)
    kz = len(plan.kz)
    dma = pltpu.SemaphoreType.DMA
    modes, sums = pl.pallas_call(
        functools.partial(middle_kernel, plan),
        grid_spec=pltpu.PrefetchScalarGridSpec(
            num_scalar_prefetch=2,
            grid=(wx + LAG,),
            in_specs=[
                pl.BlockSpec(
                    (3, 2, 1, wz, full_y),
                    lambda i, *_: (0, 0, jnp.minimum(i, wx - 1), 0, 0),
                )
            ]
            + [whole] * 18,
            out_specs=[whole, whole],
            scratch_shapes=[
                pltpu.VMEM((3, plan.slots * plan.stride, 2 * by), F32),
                pltpu.VMEM((SLABS, cols, 3, wz, 2 * by), F32),
                pltpu.VMEM((wx, 3, kz, 2 * by), F32),
                pltpu.VMEM((DEPTH, 3, NZ, 2 * by), F32),
                pltpu.VMEM((wx, 2, full_y), F32),
                pltpu.VMEM((cols, wx, 2, full_y), F32),
                dma((SLABS, cols)),
                dma((wx, cols)),
                dma((DEPTH, rows)),
                dma((plan.live,)),
                dma((cols,)),
                dma((cols,)),
                pltpu.VMEM((5, plan.slots * plan.stride, 2 * by), F32),
                pltpu.VMEM((wx, 5, NZ, 2 * by), F32),
                pltpu.VMEM((DEPTH, 5, kz, 2 * by), F32),
                pltpu.VMEM((wx, half, 5, wz, 2 * by), F32),
                pltpu.VMEM((wx, half, 5, ns, 2 * by), F32),
                pltpu.VMEM((DEPTH, 2, ns, lk), F32),
                pltpu.VMEM((wx, 2, wz, lk), F32),
                dma((DEPTH, rows)),
                dma((wx, rows)),
                dma((DEPTH, half)),
                dma((wx, half)),
                dma((DEPTH,)),
                dma((wx, half)),
                dma((DEPTH, cols)),
                dma((wx,)),
            ],
        ),
        out_shape=[
            jax.ShapeDtypeStruct((wx, 2, wz, lk), F32),
            jax.ShapeDtypeStruct((wx, 2, full_y), F32),
        ],
        compiler_params=pltpu.CompilerParams(
            dimension_semantics=("arbitrary",), vmem_limit_bytes=VMEM_BYTES,
            collective_id=0, has_side_effects=True,
        ),
    )(
        amount, real, velocity, *table["inv_y"], *table["inv_z"],
        *table["inv_x"], *table["fwd_x"], *table["fwd_z"], *side_y, table["ky"], kz_far,
    )
    state_spec = pl.BlockSpec((3, 2, 1, wz, full_y), lambda i, *_: (0, 0, i, 0, 0))
    new_velocity, new_accumulator = pl.pallas_call(
        functools.partial(last_kernel, plan),
        grid_spec=pltpu.PrefetchScalarGridSpec(
            num_scalar_prefetch=3,
            grid=(wx,),
            in_specs=[state_spec] * 2
            + [pl.BlockSpec((1, 2, wz, lk), lambda i, *_: (i, 0, 0, 0))],
            out_specs=[state_spec] * 2,
        ),
        out_shape=[jax.ShapeDtypeStruct(velocity.shape, F32)] * 2,
        compiler_params=pltpu.CompilerParams(
            dimension_semantics=("arbitrary",), vmem_limit_bytes=48 * 1024 * 1024
        ),
    )(amount, base, real, velocity, accumulator, modes)
    totals = jnp.sum(sums, axis=-1)
    stress = totals[:, 0] / (NY * NZ)
    dissipation = 2.0 * viscosity[0] * totals[:, 1] / (NY * NZ)
    return new_velocity, new_accumulator, jnp.stack([stress, dissipation])


def solution(mesh):
    state = P(None, None, "row", "col", None)
    in_specs = (state, state, P("row"), P("row"), P(), P(), P(), P())
    out_specs = (state, state, P(None, "row"))
    return jax.shard_map(
        body, mesh=mesh, in_specs=in_specs, out_specs=out_specs, check_vma=False
    )
```

time: 399 us -> 310 us (0.78)
  Pallas kernels: 389 us -> 294 us
  local copies, waits for them, and re-layouts: 0.62 us -> 5.92 us
    pallas_call x1, Pallas kernels: 364 us -> 276 us  [body(): pl.pallas_call(functools.partial(middle_kernel, plan), grid_spec=pltpu.Pr...]
    pallas_call x1, Pallas kernels: 24.5 us -> 17.1 us  [body(): pl.pallas_call(functools.partial(last_kernel, plan), grid_spec=pltpu.Pref...]
where the time goes in v3:
time: 310 us; the launch traced here: 306 us
  Pallas kernels  294 us (95%)
  local copies, waits for them, and re-layouts  5.92 us (2%)
  between operations  3.25 us (1%)
    pallas_call x1, Pallas kernels, body(): pl.pallas_call(functools.partial(middle_kernel, plan), grid_spec=pltpu.Pr...  276 us
    pallas_call x1, Pallas kernels, body(): pl.pallas_call(functools.partial(last_kernel, plan), grid_spec=pltpu.Pref...  17.1 us

profile of v3, /device:TPU:18, one launch (start us, length us, event | category | flops | bytes accessed | tf_op | source)
XLA Modules:
  0.0 305.6 jit_solution(3840983025589336367)
XLA Ops:
  3.2 0.7 concatenate.3.real
  3.9 0.0 copy-start.1
  3.9 0.1 pad_add_fusion.base
  4.0 1.2 and_select_fusion.amount
  5.2 0.0 copy-start.2
  5.2 1.6 dynamic-slice_bitcast_fusion.2.kz_far
  6.7 1.8 dynamic-slice_bitcast_fusion
  8.5 276.5 %shard_map.265 = (f32[16,2,64,384]{3,2,1,0:T(8,128)}, f32[16,2,256]{2,1,0:T(2,128)}) custom-call(s32[16]{0:T(128)} %and_select_fusion.amount, f32[5]{0:T(128)} %concatenate.3.real, f32[3,2,16,64,256]{4,3,2,1,0:T(8,128)} %vel.3, bf16[512,512]{1,0:T(8,128)(2,1)} %constant.98.clone.yh, bf16[512,512]{1,0:T(8,128)(2,1)} %constant.99.clone.yl, ...), custom_call_target="tpu_custom_call" | custom-call | tf_op jit(solution)/shard_map/pallas_call | solution.py:694
  285.0 0.8 reduce_sum.9
  285.8 0.2 fusion.2
  286.0 0.6 pad_maximum_fusion
  286.6 0.0 copy-done.1
  286.6 0.0 copy-done.2
  286.6 0.0 copy-start
  286.6 1.9 copy-done
  288.5 17.1 %shard_map.266 = (f32[3,2,16,64,256]{4,3,2,1,0:T(8,128)}, f32[3,2,16,64,256]{4,3,2,1,0:T(8,128)}) custom-call(s32[16]{0:T(128)S(1)} %copy-done.2, s32[2]{0:T(128)S(1)} %pad_add_fusion.base, f32[5]{0:T(128)S(1)} %copy-done.1, f32[3,2,16,64,256]{4,3,2,1,0:T(8,128)} %vel.3, f32[3,2,16,64,256]{4,3,2,1,0:T(8,128)} %acc.1, f32[16,2,64,384]{3,2,1,0:T(8,128)S(1)} %copy-done), custom_call_target="tpu_custom_call" | custom-call | tf_op jit(solution)/shard_map/pallas_call | solution.py:750
Async XLA Ops:
  3.9 282.7 %copy-start.1 = (f32[5]{0:T(128)S(1)}, f32[5]{0:T(128)}, u32[]{:S(2)}) copy-start(f32[5]{0:T(128)} %concatenate.3.real) | copy-start | bytes 64
  5.2 281.5 %copy-start.2 = (s32[16]{0:T(128)S(1)}, s32[16]{0:T(128)}, u32[]{:S(2)}) copy-start(s32[16]{0:T(128)} %and_select_fusion.amount) | copy-start | bytes 196
  286.6 1.9 copy-start

commit v4 on v3

--- a/solution.py
+++ b/solution.py
@@ -14,6 +14,7 @@
 NZ = 256
 LAG = 2
 AHEAD = 2
+GROUP = 2
 DEPTH = 4
 SLABS = 8
 OCT = 8
@@ -94,19 +95,10 @@
     for h in range(plan.cols):
         y = slice(h * plan.by, (h + 1) * plan.by)
         block.append(np.concatenate([lanes(cy[y], -sy[y]), lanes(sy[y], cy[y])], 0))
-    side_y = np.stack(
-        [
-            np.concatenate(
-                [block[h // plan.half * plan.half + (h + j) % plan.half] for j in range(plan.half)], 0
-            )
-            for h in range(plan.cols)
-        ]
-    )
+    side_y = np.stack(block)
     signed = np.array([j if 2 * j < NY else j - NY for j in plan.ky], np.float64)
     signed = np.pad(signed, (0, 192 - plan.ky_live))[None]
     ky = np.repeat(lanes(signed, signed), 8, 0)
-    kz = np.array([j if 2 * j < NZ else j - NZ for j in plan.kz], np.float64)
-    kz = np.repeat(kz.reshape(2, plan.side_rows, 1)[::-1], plan.lanes, 2)
     return {
         "inv_y": halves(inv_y),
         "inv_z": halves(inv_zc) + halves(inv_zs),
@@ -115,7 +107,6 @@
         "fwd_z": halves(inv_zc.T) + halves(inv_zs.T),
         "side_y": halves(side_y),
         "ky": jnp.asarray(ky, F32),
-        "kz_far": jnp.asarray(np.ascontiguousarray(kz), F32),
     }
 
 
@@ -187,7 +178,7 @@
 
 
 def backward_part(
-    plan, real, grid_in, ixh, ixl, fxh, fxl, ch, cl, sh, sl, yh, yl, ky, kz_far,
+    plan, real, grid_in, ixh, ixl, fxh, fxl, ch, cl, sh, sl, yh, yl, ky,
     out, blocks, spans, lines, near, relay, pairs, far,
     row_send, row_recv, near_send, near_recv, relay_send, relay_recv, far_send, far_recv,
 ):
@@ -364,13 +355,25 @@
 
     def transform(pieces, rows_in):
         high, low = split(jnp.concatenate([g.reshape(5 * rows_in, 2 * by) for g in pieces], 1))
-        made = dot3(high, low, yh[...], yl[...])
+        sources = [side * half + (local + j) % half for j in range(half)]
+        table_h = jnp.concatenate([yh[q] for q in sources], 0)
+        table_l = jnp.concatenate([yl[q] for q in sources], 0)
+        made = dot3(high, low, table_h, table_l)
         return [made[p * rows_in : (p + 1) * rows_in] for p in range(5)]
 
     def wave(i):
         k0 = jnp.full((1, lk), (row * wx + i).astype(F32), F32)
         return k0, ky[0:1] - real[4] * k0
 
+    def far_kz():
+        line = lax.broadcasted_iota(jnp.int32, (ns, lk), 0)
+        iz = jnp.zeros((ns, lk), jnp.int32)
+        for q, (low, n) in enumerate(plan.window):
+            first = plan.offset[q] - q // half * ns
+            here = (line >= first) & (line < first + n) & (other == q // half)
+            iz = jnp.where(here, line + (q * plan.wz + low - first), iz)
+        return jnp.where(2 * iz < NZ, iz, iz - NZ).astype(F32)
+
     def relay_step(i):
         @pl.when(col == gate)
         def _():
@@ -384,7 +387,7 @@
             mine = lines[i % DEPTH, :, pl.ds(pl.multiple_of(far_first, 8), ns), :]
             t = transform([mine] + [relay[i, j] for j in range(1, half)], ns)
             k0, k1 = wave(i)
-            first, second = reduce_modes(t, k0, k1, kz_far[...])
+            first, second = reduce_modes(t, k0, k1, far_kz())
             pairs[i % DEPTH, 0] = first
             pairs[i % DEPTH, 1] = second
             each_far(lambda h: far_copy(i, h, h).start())
@@ -453,7 +456,7 @@
 
 def middle_kernel(
     plan, amount, real, vel, yh, yl, ch, cl, sh, sl,
-    ixh, ixl, fxh, fxl, bch, bcl, bsh, bsl, byh, byl, ky, kz_far,
+    ixh, ixl, fxh, fxl, bch, bcl, bsh, bsl, byh, byl, ky,
     out, sums, grid_in, part, lines, spans, own, parts,
     col_send, col_recv, row_send, row_recv, sum_send, sum_recv, *back,
 ):
@@ -599,7 +602,7 @@
         lax.fori_loop(0, plan.live, arrived, 0)
         backward_part(
             plan, real, grid_in, ixh, ixl, fxh, fxl, bch, bcl, bsh, bsl, byh, byl, ky,
-            kz_far, out, *back
+            out, *back
         )
 
         def sent(i, carry):
@@ -640,21 +643,22 @@
     return rows
 
 
-def last_kernel(plan, amount, base, real, vel, acc, modes, new_vel, new_acc):
+def update_row(m, plan, amount, base, real, vel, acc, modes, new_vel, new_acc):
     shape = vel.shape[3:]
-    kx = base[0] + pl.program_id(0)
+    index = pl.program_id(0) * GROUP + m
+    kx = base[0] + index
     k, ksq, inv, keep = geometry(kx, base[1], real, shape)
-    shift = amount[pl.program_id(0)]
+    shift = amount[index]
     viscosity, shear, step = real[0], real[1], real[3]
     coupling = 2.0 * shear * k[0] * inv
     h2 = k[0] * k[0] + k[2] * k[2]
     flat = h2 == 0.0
     ih2 = 1.0 / jnp.maximum(h2, 1.0)
-    firsts = spread(modes[0, 0], plan)
-    seconds = spread(modes[0, 1], plan)
+    firsts = spread(modes[m, 0], plan)
+    seconds = spread(modes[m, 1], plan)
     for p in range(2):
-        v = [pltpu.roll(vel[c, p, 0], shift, 1) for c in range(3)]
-        old = [pltpu.roll(acc[c, p, 0], shift, 1) for c in range(3)]
+        v = [pltpu.roll(vel[c, p, m], shift, 1) for c in range(3)]
+        old = [pltpu.roll(acc[c, p, m], shift, 1) for c in range(3)]
         sign = 1.0 if p == 0 else -1.0
         a = jnp.where(keep, sign * firsts[1 - p], 0.0)
         b = jnp.where(keep, sign * seconds[1 - p], 0.0)
@@ -671,8 +675,13 @@
             if c == 0:
                 rate = rate - shear * v[1]
             total = (-5.0 / 9.0) * old[c] + step * rate
-            new_acc[c, p, 0] = total
-            new_vel[c, p, 0] = v[c] + (15.0 / 16.0) * total
+            new_acc[c, p, m] = total
+            new_vel[c, p, m] = v[c] + (15.0 / 16.0) * total
+
+
+def last_kernel(plan, *refs):
+    for m in range(GROUP):
+        update_row(m, plan, *refs)
 
 
 def body(velocity, accumulator, remesh_flag, remesh_shift, viscosity, shear, clock, step):
@@ -686,8 +695,6 @@
     col = lax.axis_index("col")
     base = jnp.stack([lax.axis_index("row") * wx, col * wz]).astype(jnp.int32)
     real = jnp.concatenate([viscosity, shear, clock, step, shear * clock])
-    side_y = [lax.dynamic_index_in_dim(t, col, 0, False) for t in table["side_y"]]
-    kz_far = lax.dynamic_index_in_dim(table["kz_far"], col // half, 0, False)
     whole = pl.BlockSpec(memory_space=pltpu.VMEM)
     kz = len(plan.kz)
     dma = pltpu.SemaphoreType.DMA
@@ -702,7 +709,7 @@
                     lambda i, *_: (0, 0, jnp.minimum(i, wx - 1), 0, 0),
                 )
             ]
-            + [whole] * 18,
+            + [whole] * 17,
             out_specs=[whole, whole],
             scratch_shapes=[
                 pltpu.VMEM((3, plan.slots * plan.stride, 2 * by), F32),
@@ -744,21 +751,21 @@
         ),
     )(
         amount, real, velocity, *table["inv_y"], *table["inv_z"],
-        *table["inv_x"], *table["fwd_x"], *table["fwd_z"], *side_y, table["ky"], kz_far,
+        *table["inv_x"], *table["fwd_x"], *table["fwd_z"], *table["side_y"], table["ky"],
     )
-    state_spec = pl.BlockSpec((3, 2, 1, wz, full_y), lambda i, *_: (0, 0, i, 0, 0))
+    state_spec = pl.BlockSpec((3, 2, GROUP, wz, full_y), lambda i, *_: (0, 0, i, 0, 0))
     new_velocity, new_accumulator = pl.pallas_call(
         functools.partial(last_kernel, plan),
         grid_spec=pltpu.PrefetchScalarGridSpec(
             num_scalar_prefetch=3,
-            grid=(wx,),
+            grid=(wx // GROUP,),
             in_specs=[state_spec] * 2
-            + [pl.BlockSpec((1, 2, wz, lk), lambda i, *_: (i, 0, 0, 0))],
+            + [pl.BlockSpec((GROUP, 2, wz, lk), lambda i, *_: (i, 0, 0, 0))],
             out_specs=[state_spec] * 2,
         ),
         out_shape=[jax.ShapeDtypeStruct(velocity.shape, F32)] * 2,
         compiler_params=pltpu.CompilerParams(
-            dimension_semantics=("arbitrary",), vmem_limit_bytes=48 * 1024 * 1024
+            dimension_semantics=("arbitrary",), vmem_limit_bytes=VMEM_BYTES
         ),
     )(amount, base, real, velocity, accumulator, modes)
     totals = jnp.sum(sums, axis=-1)

time: 310 us -> 304 us (0.981)
  local copies, waits for them, and re-layouts: 5.92 us -> 0.57 us
    squeeze x2 -> x0, local copies, waits for them, and re-layouts: 3.36 us -> none  [the longest x1 1.8 us: body(): lax.dynamic_index_in_dim(t, col, 0, False)]
where the time goes in v4:
time: 304 us; the launch traced here: 300 us
  Pallas kernels  292 us (96%)
  other arithmetic  3.47 us (1%)
  between operations  3.24 us (1%)
    pallas_call x1, Pallas kernels, body(): pl.pallas_call(functools.partial(middle_kernel, plan), grid_spec=pltpu.Pr...  277 us
    pallas_call x1, Pallas kernels, body(): pl.pallas_call(functools.partial(last_kernel, plan), grid_spec=pltpu.Pref...  15.7 us

profile of v4, /device:TPU:18, one launch (start us, length us, event | category | flops | bytes accessed | tf_op | source)
XLA Modules:
  0.0 299.5 jit_solution(4673466566748444681)
XLA Ops:
  3.2 0.6 concatenate.3.real.refs_2_
  3.8 0.6 pad_add_fusion.refs_1_
  4.4 1.3 and_select_fusion.amount.refs_0_
  5.7 276.6 %shard_map.256 = (f32[16,2,64,384]{3,2,1,0:T(8,128)}, f32[16,2,256]{2,1,0:T(2,128)}) custom-call(s32[16]{0:T(128)} %and_select_fusion.amount.refs_0_, f32[5]{0:T(128)} %concatenate.3.real.refs_2_, f32[3,2,16,64,256]{4,3,2,1,0:T(8,128)} %refs_3_.1, bf16[512,512]{1,0:T(8,128)(2,1)} %constant.71.clone.yh, bf16[512,512]{1,0:T(8,128)(2,1)} %constant.72.clone.yl, ...), custom_call_target="tpu_custom_call" | custom-call | tf_op jit(solution)/shard_map/pallas_call | solution.py:701
  282.2 0.8 reduce_sum.9
  283.1 0.2 fusion.2
  283.3 0.6 pad_maximum_fusion
  283.8 15.7 %shard_map.257 = (f32[3,2,16,64,256]{4,3,2,1,0:T(8,128)}, f32[3,2,16,64,256]{4,3,2,1,0:T(8,128)}) custom-call(s32[16]{0:T(128)} %and_select_fusion.amount.refs_0_, s32[2]{0:T(128)} %pad_add_fusion.refs_1_, f32[5]{0:T(128)} %concatenate.3.real.refs_2_, f32[3,2,16,64,256]{4,3,2,1,0:T(8,128)} %refs_3_.1, f32[3,2,16,64,256]{4,3,2,1,0:T(8,128)} %refs_4_.1, ...), custom_call_target="tpu_custom_call" | custom-call | tf_op jit(solution)/shard_map/pallas_call | solution.py:757
